TPU v7x, 128 devices: a whole 4x4x4 slice. The times are simulated.
128 devices in a mesh: dp: 128 (over x, z, y, core).
Axes of the slice: x: 4, y: 4, z: 4, core: 2. Of those that a mesh axis runs over, the one named last changes fastest.
Arguments:
- captions: bfloat16 [4096, 77, 768], P('dp'), may hold values from -6 to 6
- caption_layout: int32 [2, 4096], replicated, may hold values from 0 to 77, as said below
- images: bfloat16 [4096, 768], P('dp'), may hold values from -0.24 to 0.24
- w_query: bfloat16 [768, 768], replicated, may hold values from -0.21875 to 0.21875
- w_keyval: bfloat16 [768, 1536], replicated, may hold values from -0.21875 to 0.21875
- w_out: bfloat16 [768, 768], replicated, may hold values from -0.21875 to 0.21875
- w_up: bfloat16 [768, 3072], replicated, may hold values from -0.21875 to 0.21875
- w_down: bfloat16 [3072, 768], replicated, may hold values from -0.109375 to 0.109375
- w_proj: bfloat16 [768, 768], replicated, may hold values from -0.009114583 to 0.009114583
Outputs:
- image_grad: float32 [4096, 768], P('dp')
- text_grad: float32 [4096, 768], P('dp')
Inputs may be any that keep to these rules, and one draw needn't show every extreme that they name: `caption_layout`: row 0 holds each caption's token count; row 1 is 1 where the caption is encoded by the next index of dp (index 0 after the last) and 0 where by its own. Exactly 8 of each device's captions carry 1. The captions one device encodes (its own that carry 0 and those carrying 1 of the index before it) hold at most 2048 tokens together, exactly that many on some device.
All inputs are finite; a program needn't handle non-finite values.
Results may differ from a plain program's by a relative error of at most 0.018.
Values may be sent and summed in bfloat16 or wider, within the bound.
A program may use at most 128 MiB of HBM per device.

v0:
```python
import math

import jax
import jax.numpy as jnp
from jax import lax
from jax.sharding import PartitionSpec as P

HEADS = 12


LOGIT_SCALE = 100.0
EPS_NORM = 1e-05
EPS_UNIT = 1e-06


def turned_gather(arrays, axis, dims):
    turned = [jnp.moveaxis(a, dim, 0) for a, dim in zip(arrays, dims)]
    both = jnp.concatenate([t.reshape(len(t), -1) for t in turned], axis=1)
    out, at, gathered = (lax.all_gather(both, axis, axis=0, tiled=True), 0, [])
    for t, dim in zip(turned, dims):
        share = out[:, at : at + t[0].size].reshape(-1, *t.shape[1:])
        gathered.append(jnp.moveaxis(share, 0, dim))
        at += t[0].size
    return tuple(gathered)


def layer_norm(values):
    values = values.astype(jnp.float32)
    center = values - jnp.mean(values, axis=-1, keepdims=True)
    spread = jnp.mean(center * center, axis=-1, keepdims=True)
    return center * lax.rsqrt(spread + EPS_NORM)


def unit_rows(values):
    values = values.astype(jnp.float32)
    return values * lax.rsqrt(jnp.sum(values * values, axis=-1, keepdims=True) + EPS_UNIT)


def contract_first(left, right):
    return lax.dot_general(
        left, right, (((0,), (0,)), ((), ())), preferred_element_type=jnp.float32
    )


def contract_last(left, right):
    return lax.dot_general(
        left, right, (((1,), (1,)), ((), ())), preferred_element_type=jnp.float32
    )


def encode(token_rows, slot_starts, slot_lengths, weight_set):
    w_query, w_keyval, w_out, w_up, w_down, w_proj = weight_set
    total_rows, model_width = token_rows.shape
    head_dim = model_width // HEADS
    normed = layer_norm(token_rows).astype(jnp.bfloat16)
    keyval = jnp.dot(normed, w_keyval, preferred_element_type=jnp.float32).astype(jnp.bfloat16)
    last_row = jnp.clip(slot_starts + slot_lengths - 1, 0, total_rows - 1)
    query = jnp.dot(normed[last_row], w_query, preferred_element_type=jnp.float32).astype(
        jnp.bfloat16
    )
    key_heads = keyval[:, :model_width].reshape(total_rows, HEADS, head_dim)
    value_heads = keyval[:, model_width:].reshape(total_rows, HEADS, head_dim)
    query_heads = query.reshape(-1, HEADS, head_dim)
    scores = jnp.einsum("shd,rhd->hsr", query_heads, key_heads, preferred_element_type=jnp.float32)
    scores = scores / math.sqrt(head_dim)
    position = jnp.arange(total_rows)[None, :]
    inside = (position >= slot_starts[:, None]) & (position < (slot_starts + slot_lengths)[:, None])
    inside = jnp.where(slot_lengths[:, None] > 0, inside, position == 0)
    masked = jnp.where(inside[None], scores, -jnp.inf)
    peak = jnp.max(masked, axis=-1, keepdims=True)
    exponent = jnp.exp(masked - peak)
    attention = (exponent / jnp.sum(exponent, axis=-1, keepdims=True)).astype(jnp.bfloat16)
    mixed_heads = jnp.einsum(
        "hsr,rhd->shd", attention, value_heads, preferred_element_type=jnp.float32
    )
    mixed_heads = mixed_heads.astype(jnp.bfloat16).reshape(-1, model_width)
    residual = token_rows[last_row].astype(jnp.float32) + jnp.dot(
        mixed_heads, w_out, preferred_element_type=jnp.float32
    )
    residual = residual.astype(jnp.bfloat16)
    inner_norm = layer_norm(residual).astype(jnp.bfloat16)
    hidden = jax.nn.gelu(
        jnp.dot(inner_norm, w_up, preferred_element_type=jnp.float32), approximate=False
    )
    hidden = hidden.astype(jnp.bfloat16)
    final_rows = residual.astype(jnp.float32) + jnp.dot(
        hidden, w_down, preferred_element_type=jnp.float32
    )
    pooled = layer_norm(final_rows).astype(jnp.bfloat16)
    return jnp.dot(pooled, w_proj, preferred_element_type=jnp.float32).astype(jnp.bfloat16)


def body(captions, caption_layout, images, w_query, w_keyval, w_out, w_up, w_down, w_proj):
    caption_count, context, model_width = captions.shape
    embed_width = images.shape[1]
    device_index = lax.axis_index("dp")
    weight_set = (w_query, w_keyval, w_out, w_up, w_down, w_proj)
    own_lengths = lax.dynamic_slice_in_dim(
        caption_layout[0], device_index * caption_count, caption_count
    )
    image_unit = unit_rows(images).astype(jnp.bfloat16)
    token_rows = captions.reshape(-1, model_width)
    own_text = encode(token_rows, jnp.arange(caption_count) * context, own_lengths, weight_set)
    text_unit = unit_rows(own_text).astype(jnp.bfloat16)
    both_rows = lax.all_gather(
        jnp.concatenate([image_unit, text_unit], axis=1), "dp", axis=0, tiled=True
    )
    all_images = both_rows[:, :embed_width]
    all_texts = both_rows[:, embed_width:]
    row_scores = LOGIT_SCALE * contract_last(image_unit, all_texts)
    column_scores = LOGIT_SCALE * contract_last(all_images, text_unit)
    row_peak = jnp.max(row_scores, axis=1, keepdims=True)
    row_logsum = row_peak[:, 0] + jnp.log(jnp.sum(jnp.exp(row_scores - row_peak), axis=1))
    column_peak = jnp.max(column_scores, axis=0, keepdims=True)
    column_logsum = column_peak[0] + jnp.log(jnp.sum(jnp.exp(column_scores - column_peak), axis=0))
    row_weights = jnp.exp(row_scores - row_logsum[:, None]).astype(jnp.bfloat16)
    column_weights = jnp.exp(column_scores - column_logsum[None, :]).astype(jnp.bfloat16)
    half_scale = 0.5 * LOGIT_SCALE
    image_unit_grad = half_scale * jnp.dot(
        row_weights, all_texts, preferred_element_type=jnp.float32
    )
    image_unit_grad = image_unit_grad - LOGIT_SCALE * text_unit.astype(jnp.float32)
    text_unit_grad = half_scale * contract_first(column_weights, all_images)
    text_unit_grad = text_unit_grad - LOGIT_SCALE * image_unit.astype(jnp.float32)
    row_every, column_every = turned_gather((row_logsum, column_logsum), "dp", (0, 0))
    cross_rows = jnp.exp(row_scores - column_every[None, :]).astype(jnp.bfloat16)
    cross_columns = jnp.exp(column_scores - row_every[:, None]).astype(jnp.bfloat16)
    image_unit_grad = image_unit_grad + half_scale * jnp.dot(
        cross_rows, all_texts, preferred_element_type=jnp.float32
    )
    text_unit_grad = text_unit_grad + half_scale * contract_first(cross_columns, all_images)
    image_value, image_back = jax.vjp(unit_rows, images.astype(jnp.float32))
    text_value, text_back = jax.vjp(unit_rows, own_text.astype(jnp.float32))
    return (image_back(image_unit_grad)[0], text_back(text_unit_grad)[0])


def solution(mesh):
    return jax.shard_map(
        body,
        mesh=mesh,
        in_specs=(P("dp", None, None), P(), P("dp", None), P(), P(), P(), P(), P(), P()),
        out_specs=(P("dp", None), P("dp", None)),
        check_vma=False,
    )
```

profile of v0, /device:TPU:1, one launch (start us, length us, event | category | flops | bytes accessed | tf_op | source)
XLA Modules:
  0.0 233.9 jit_solution(17604670309466360068)
XLA Ops:
  7.2 0.9 slice.21
  8.2 0.7 bitcast_compare_fusion
  8.8 0.1 fusion.112
  8.9 0.7 bitcast_add_fusion
  9.6 2.6 %convert_reduce_fusion = f32[32,77]{0,1:T(8,128)S(1)} fusion(bf16[32,77,768]{2,0,1:T(8,128)(2,1)} %param.9), kind=kLoop, calls=%fused_computation.5 | loop fusion | flops 3782240 | bytes 3794560 | tf_op jit(solution)/shard_map/reduce_sum | solution.py:29
  12.3 0.1 div.47
  12.4 0.1 copy.32
  12.5 6.2 %copy.30 = bf16[32,77,768]{2,1,0:T(8,128)(2,1)} copy(bf16[32,77,768]{2,0,1:T(8,128)(2,1)} %param.9) | data formatting | bytes 7569408 | tf_op args[0]
  18.7 0.1 fusion.101
  18.8 0.5 copy-done.16
  19.4 1.2 fusion.2
  20.7 0.7 rsqrt.51
  21.4 0.7 fusion.102
  22.1 5.0 %reshape.265 = bf16[2464,768]{1,0:T(8,128)(2,1)} reshape(bf16[32,77,768]{2,1,0:T(8,128)(2,1)} %copy.30) | data formatting | bytes 7569408 | tf_op jit(solution)/shard_map/reshape | solution.py:102
  27.1 3.8 %gather_fusion = bf16[32,768]{1,0:T(8,128)(2,1)} fusion(bf16[2464,768]{1,0:T(8,128)(2,1)} %reshape.265, s32[1024]{0:T(1024)S(1)} %pad_clamp_fusion), kind=kCustom, calls=%fused_computation | custom fusion | bytes 98432 | tf_op jit(solution)/shard_map/gather | solution.py:77
  30.9 4.9 %multiply_convert_fusion = bf16[2464,768]{1,0:T(8,128)(2,1)} fusion(bf16[2464,768]{1,0:T(8,128)(2,1)} %reshape.265, f32[2464]{0:T(1024)} %rsqrt.51, f32[2464]{0:T(1024)S(1)} %div.47), kind=kLoop, calls=%fused_computation.8 | loop fusion | flops 7569408 | bytes 7589120 | tf_op jit(solution)/shard_map/convert_element_type | solution.py:55
  35.8 4.0 %gather_fusion.1 = bf16[32,768]{1,0:T(8,128)(2,1)} fusion(bf16[2464,768]{1,0:T(8,128)(2,1)} %multiply_convert_fusion, s32[1024]{0:T(1024)} %copy-done.11), kind=kCustom, calls=%fused_computation.1 | custom fusion | bytes 98432 | tf_op jit(solution)/shard_map/gather | solution.py:58
  39.7 1.7 convolution_convert_fusion.2
  41.5 0.9 reshape.267
  42.4 8.4 %convolution_convert_fusion = bf16[2464,1536]{1,0:T(8,128)(2,1)S(1)} fusion(bf16[2464,768]{1,0:T(8,128)(2,1)} %multiply_convert_fusion, bf16[768,1536]{1,0:T(8,128)(2,1)S(1)} %copy-done), kind=kOutput, calls=%fused_computation.3 | convolution fusion | flops 5817090048 | bytes 13713408 | tf_op jit(solution)/shard_map/dot_general | solution.py:56
  50.8 3.4 %fusion.146 = (bf16[2464,768]{1,0:T(8,128)(2,1)}, bf16[2464,768]{1,0:T(8,128)(2,1)}) fusion(bf16[2464,1536]{1,0:T(8,128)(2,1)S(1)} %convolution_convert_fusion), kind=kLoop, calls=%fused_computation.187 | loop fusion | bytes 15138816 | tf_op jit(solution)/shard_map/slice | solution.py:61
  54.2 6.1 %copy.35 = bf16[2464,768]{0,1:T(8,128)(2,1)} copy(bf16[2464,768]{1,0:T(8,128)(2,1)} %get-tuple-element.2) | data formatting | bytes 7569408 | tf_op jit(solution)/shard_map/slice | solution.py:61
  60.3 0.2 fusion.65
  60.5 2.9 %fusion.16 = f32[12,32,2464]{2,1,0:T(8,128)S(1)} fusion(bf16[2464,12,64]{0,2,1:T(8,128)(2,1)} %bitcast.40, pred[32,2464]{1,0:T(8,128)(4,1)S(1)} %fusion.65, bf16[32,12,64]{2,1,0:T(8,128)(2,1)S(1)} %reshape.267), kind=kOutput, calls=%fused_computation.23 | convolution fusion | flops 123002880 | bytes 7697408 | tf_op jit(solution)/shard_map/shd,rhd->hsr/dot_general | solution.py:64
  63.4 1.9 copy-done.3
  65.3 0.8 fusion.148
  66.1 6.1 %copy.34 = bf16[2464,768]{0,1:T(8,128)(2,1)} copy(bf16[2464,768]{1,0:T(8,128)(2,1)} %get-tuple-element.3) | data formatting | bytes 7569408 | tf_op jit(solution)/shard_map/slice | solution.py:62
  72.1 5.7 %fusion.26 = bf16[32,12,64]{2,0,1:T(8,128)(2,1)S(1)} fusion(bf16[2464,12,64]{0,2,1:T(8,128)(2,1)} %bitcast.41, f32[12,32]{1,0:T(8,128)S(1)} %fusion.148, f32[12,32,2464]{2,1,0:T(8,128)} %copy-done.3), kind=kOutput, calls=%fused_computation.30 | convolution fusion | flops 123976480 | bytes 7620096 | tf_op jit(solution)/shard_map/hsr,rhd->shd/dot_general | solution.py:73
  78.0 0.1 reshape.269
  78.1 0.4 fusion.149
  78.5 0.2 multiply_reduce_fusion.3
  78.8 6.2 %fusion.150 = (f32[32]{0:T(128)S(1)}, f32[32,768]{1,0:T(8,128)S(1)}) fusion(f32[32,768]{1,0:T(8,128)S(1)} %get-tuple-element.7, bf16[3072,768]{1,0:T(8,128)(2,1)} %param.16, bf16[768,3072]{1,0:T(8,128)(2,1)} %param.15, f32[32]{0:T(128)S(1)} %add_rsqrt_fusion.2, f32[32]{0:T(128)S(1)} %broadcast_multiply_fusion.2), kind=kOutput, calls=%fused_computation.191 | convolution fusion | flops 308502496 | bytes 9634176 | tf_op jit(solution)/shard_map/dot_general | solution.py:86
  85.0 0.2 multiply_reduce_fusion.2
  85.2 0.5 multiply_reduce_fusion.1
  85.8 0.6 pad_maximum_fusion
  86.4 76.8 %all-gather.3.cloned.1.call-done = bf16[4096,1536]{1,0:T(8,128)(2,1)} async-done(((bf16[32,1536]{1,0:T(8,128)(2,1)}), bf16[4096,1536]{1,0:T(8,128)(2,1)}) %all-gather.3.cloned.1.call-update) | async-done | bytes 12582928 | tf_op jit(solution)/shard_map/all_gather | solution.py:105
  163.2 4.8 %fusion.152 = (f32[32]{0:T(128)S(1)}, f32[4096,32]{0,1:T(8,128)S(1)}) fusion(bf16[32,768]{1,0:T(8,128)(2,1)S(1)} %multiply_convert_fusion.1, bf16[4096,1536]{1,0:T(8,128)(2,1)} %all-gather.3.cloned.1.call-done), kind=kOutput, calls=%fused_computation.193 | convolution fusion | flops 201588704 | bytes 6865024 | tf_op jit(solution)/shard_map/dot_general | solution.py:46
  168.1 0.3 exponential_reduce_fusion
  168.3 4.8 %fusion.151 = (f32[32]{0:T(128)S(1)}, f32[32,4096]{1,0:T(8,128)S(1)}) fusion(bf16[32,768]{1,0:T(8,128)(2,1)S(1)} %copy-done.7, bf16[4096,1536]{1,0:T(8,128)(2,1)} %all-gather.3.cloned.1.call-done), kind=kOutput, calls=%fused_computation.192 | convolution fusion | flops 201588704 | bytes 6865024 | tf_op jit(solution)/shard_map/dot_general | solution.py:46
  173.2 0.3 exponential_reduce_fusion.1
  173.5 35.6 %all-gather = f32[128,32,2]{1,2,0:T(2,128)S(1)} all-gather(f32[1,32,2]{1,2,0:T(2,128)S(1)} %maximum_bitcast_fusion), channel_id=1, replica_groups=mesh['dp'=128] {'dp'}, dimensions={0}, use_global_device_ids=true | all-gather | bytes 33024 | tf_op jit(solution)/shard_map/all_gather | solution.py:19
  209.1 0.1 reshape.287
  209.2 4.0 %fusion.42 = f32[32,768]{1,0:T(8,128)S(1)} fusion(bf16[4096,1536]{1,0:T(8,128)(2,1)} %all-gather.3.cloned.1.call-done, f32[4096,32]{0,1:T(8,128)S(1)} %get-tuple-element.15, f32[32]{0:T(128)S(1)} %log_add_fusion, bf16[32,768]{1,0:T(8,128)(2,1)S(1)} %copy-done.7), kind=kOutput, calls=%fused_computation.38 | convolution fusion | flops 201687040 | bytes 6963328 | tf_op jit(solution)/shard_map/dot_general | solution.py:40
  213.2 4.1 %multiply_reduce_fusion = (f32[32]{0:T(128)S(1)}, f32[32,768]{1,0:T(8,128)S(1)}) fusion(f32[32,768]{1,0:T(8,128)S(1)} %get-tuple-element.11, f32[32,768]{1,0:T(8,128)S(1)} %fusion.42, bf16[4096,1536]{1,0:T(8,128)(2,1)} %all-gather.3.cloned.1.call-done, f32[4096,32]{0,1:T(8,128)S(1)} %get-tuple-element.15, f32[4096]{0:T(1024)S(1)} %bitcast.42), kind=kOutput, calls=%fused_computation.120 | convolution fusion | flops 201687008 | bytes 7127168 | tf_op jit(solution)/shard_map/dot_general | solution.py:40
  217.3 4.2 %fusion.48 = f32[32,768]{1,0:T(8,128)S(1)} fusion(bf16[4096,1536]{1,0:T(8,128)(2,1)} %all-gather.3.cloned.1.call-done, f32[32,4096]{1,0:T(8,128)S(1)} %get-tuple-element.13, f32[32]{0:T(128)S(1)} %log_add_fusion.1, bf16[32,768]{1,0:T(8,128)(2,1)S(1)} %multiply_convert_fusion.1), kind=kOutput, calls=%fused_computation.40 | convolution fusion | flops 201687040 | bytes 6963328 | tf_op jit(solution)/shard_map/dot_general | solution.py:119
  221.6 4.1 %fusion.103 = (f32[32]{0:T(128)S(1)}, f32[32,768]{1,0:T(8,128)S(1)}) fusion(bf16[32,768]{1,0:T(8,128)(2,1)S(1)} %copy-done.9, f32[32,768]{1,0:T(8,128)S(1)} %fusion.48, bf16[4096,1536]{1,0:T(8,128)(2,1)} %all-gather.3.cloned.1.call-done, f32[32,4096]{1,0:T(8,128)S(1)} %get-tuple-element.13, f32[4096]{0:T(1024)S(1)} %bitcast.43), kind=kOutput, calls=%fused_computation.117 | convolution fusion | flops 201711584 | bytes 7078016 | tf_op jit(solution)/shard_map/dot_general | solution.py:128
  225.6 0.7 add_add_fusion
  226.4 0.7 add_add_fusion.1
  (59 shorter events, 0.6 us)
Async XLA Ops:
  7.2 35.3 %copy-start = (bf16[768,1536]{1,0:T(8,128)(2,1)S(1)}, bf16[768,1536]{1,0:T(8,128)(2,1)}, u32[]{:S(2)}) copy-start(bf16[768,1536]{1,0:T(8,128)(2,1)} %param.13) | copy-start | bytes 7077892
  7.2 156.1 %all-gather.3.cloned.1.call-start = ((), (), s32[]{:S(2)}) async-start(), calls=%async_computation | async-start | bytes 12681216 | tf_op jit(solution)/shard_map/all_gather | solution.py:105
  12.2 6.5 %copy-start.8 = (bf16[32,768]{1,0:T(8,128)(2,1)S(1)}, bf16[32,768]{1,0:T(8,128)(2,1)}, u32[]{:S(2)}) copy-start(bf16[32,768]{1,0:T(8,128)(2,1)} %param.11) | copy-start | bytes 147460
  12.5 6.9 %copy-start.2 = (bf16[32,77,768]{2,0,1:T(8,128)(2,1)S(1)}, bf16[32,77,768]{2,0,1:T(8,128)(2,1)}, u32[]{:S(2)}) copy-start(bf16[32,77,768]{2,0,1:T(8,128)(2,1)} %param.9) | copy-start | bytes 11354116
  18.8 0.5 copy-start.16
  19.4 7.7 %copy-start.12 = (f32[32]{0:T(128)}, f32[32]{0:T(128)S(1)}, u32[]{:S(2)}) copy-start(f32[32]{0:T(128)S(1)} %add_rsqrt_fusion.4) | copy-start | bytes 388
  19.4 7.7 %copy-start.11 = (s32[1024]{0:T(1024)}, s32[1024]{0:T(1024)S(1)}, u32[]{:S(2)}) copy-start(s32[1024]{0:T(1024)S(1)} %pad_clamp_fusion) | copy-start | bytes 12292
  30.9 8.8 %copy-start.4 = (bf16[768,768]{1,0:T(8,128)(2,1)S(1)}, bf16[768,768]{1,0:T(8,128)(2,1)}, u32[]{:S(2)}) copy-start(bf16[768,768]{1,0:T(8,128)(2,1)} %param.12) | copy-start | bytes 3538948
  54.2 6.1 %copy-start.14 = (s32[32]{0:T(128)S(1)}, s32[32]{0:T(128)}, u32[]{:S(2)}) copy-start(s32[32]{0:T(128)} %get-tuple-element.20) | copy-start | bytes 388
  54.2 6.1 %copy-start.15 = (s32[32]{0:T(128)S(1)}, s32[32]{0:T(128)}, u32[]{:S(2)}) copy-start(s32[32]{0:T(128)} %get-tuple-element.21) | copy-start | bytes 388
  54.2 6.1 %copy-start.18 = (pred[32]{0:T(512)(128)(4,1)S(1)}, pred[32]{0:T(512)(128)(4,1)}, u32[]{:S(2)}) copy-start(pred[32]{0:T(512)(128)(4,1)} %bitcast_compare_fusion) | copy-start | bytes 100
  63.4 1.9 copy-start.3
  72.1 5.9 %copy-start.5 = (bf16[768,768]{1,0:T(8,128)(2,1)S(1)}, bf16[768,768]{1,0:T(8,128)(2,1)}, u32[]{:S(2)}) copy-start(bf16[768,768]{1,0:T(8,128)(2,1)} %param.14) | copy-start | bytes 3538948
  72.1 5.9 %copy-start.10 = (bf16[32,768]{1,0:T(8,128)(2,1)S(1)}, bf16[32,768]{1,0:T(8,128)(2,1)}, u32[]{:S(2)}) copy-start(bf16[32,768]{1,0:T(8,128)(2,1)} %gather_fusion) | copy-start | bytes 147460
  78.8 6.4 %copy-start.6 = (bf16[768,768]{1,0:T(8,128)(2,1)S(1)}, bf16[768,768]{1,0:T(8,128)(2,1)}, u32[]{:S(2)}) copy-start(bf16[768,768]{1,0:T(8,128)(2,1)} %param.17) | copy-start | bytes 3538948
  78.8 7.0 %copy-start.7 = (bf16[32,768]{1,0:T(8,128)(2,1)S(1)}, bf16[32,768]{1,0:T(8,128)(2,1)}, u32[]{:S(2)}) copy-start(bf16[32,768]{1,0:T(8,128)(2,1)} %fusion.102) | copy-start | bytes 147460
  217.3 4.2 %copy-start.9 = (bf16[32,768]{1,0:T(8,128)(2,1)S(1)}, bf16[32,768]{1,0:T(8,128)(2,1)}, u32[]{:S(2)}) copy-start(bf16[32,768]{1,0:T(8,128)(2,1)} %param.11) | copy-start | bytes 147460
  217.3 9.8 %copy-start.1 = (bf16[768,1536]{1,0:T(8,128)(2,1)S(1)}, bf16[768,1536]{1,0:T(8,128)(2,1)}, u32[]{:S(2)}) copy-start(bf16[768,1536]{1,0:T(8,128)(2,1)} %param.13) | copy-start | bytes 7077892
  221.5 4.1 %copy-start.17 = (f32[32]{0:T(128)S(1)}, f32[32]{0:T(128)}, u32[]{:S(2)}) copy-start(f32[32]{0:T(128)} %copy-done.16) | copy-start | bytes 388
  221.5 4.8 %copy-start.13 = (f32[32]{0:T(128)S(1)}, f32[32]{0:T(128)}, u32[]{:S(2)}) copy-start(f32[32]{0:T(128)} %copy-done.12) | copy-start | bytes 388
Sparse Core Ops, SparseCore 0:
  86.5 76.6 all-gather.2
where the time goes:
time: 235 us; the launch traced here: 234 us
  waiting for transfers between devices  76.8 us (33%)
  matrix products  51.8 us (22%)
  local copies, waits for them, and re-layouts  40.3 us (17%)
  blocking collectives  35.6 us (15%)
  other arithmetic  15 us (6%)
  between operations  14.4 us (6%)
    all_gather x1, waiting for transfers between devices, body(): lax.all_gather(jnp.concatenate([image_unit, text_unit], axis=1), 'dp', ax...  76.8 us
    all_gather x1, blocking collectives, turned_gather(): out, at, gathered = (lax.all_gather(both, axis, axis=0, tiled=True), 0, [])  35.6 us
    dot_general x2, matrix products, contract_last(): lax.dot_general(left, right, (((1,), (1,)), ((), ())), preferred_element_...  9.66 us
    slice x2, local copies, waits for them, and re-layouts, encode(): key_heads = keyval[:, :model_width].reshape(total_rows, HEADS, head_dim)  9.47 us
    unnamed x40, local copies, waits for them, and re-layouts  8.83 us
    dot_general x1, matrix products, encode(): jnp.dot(normed, w_keyval, preferred_element_type=jnp.float32)  8.36 us
    dot_general x2, matrix products, contract_first(): lax.dot_general(left, right, (((0,), (0,)), ((), ())), preferred_element_...  8.07 us
    dot_general x1, matrix products, encode(): jnp.dot(hidden, w_down, preferred_element_type=jnp.float32)  6.17 us
  transfers between devices with their start and end apart: 1, of which 1 were waited for; matrix products, arithmetic and copies ran while one was open for 0% of the time, Pallas kernels for 0%

commit v1 on v0

v1 whole, which is shorter than its diff:
```python
import math

import jax
import jax.numpy as jnp
from jax import lax
from jax.experimental import pallas as pl
from jax.experimental.pallas import tpu as pltpu
from jax.sharding import PartitionSpec as P

HEADS = 12
HEAD_DIM = 64
WIDTH = 768
CTX = 77
CAPS = 32
FF = 3072
GROUP = 16
GROUPS = CAPS // GROUP
COLS = HEADS * GROUP
TOKENS = CTX * GROUP
LOAD_STEPS = 7
STEP_T = CTX // LOAD_STEPS
CHIPS = 8
ROWS = CHIPS * 2 * CAPS
CHUNK = 128
CHUNKS = ROWS // CHUNK

LOGIT_SCALE = 100.0
EPS_NORM = 1e-05
EPS_UNIT = 1e-06

MESH = pl.DeviceIdType.MESH
F32 = jnp.float32
BF16 = jnp.bfloat16


def norm_rows(values):
    center = values - jnp.mean(values, axis=-1, keepdims=True)
    spread = jnp.mean(center * center, axis=-1, keepdims=True)
    return center * lax.rsqrt(spread + EPS_NORM)


def unit_scale(values):
    return lax.rsqrt(jnp.sum(values * values, axis=-1, keepdims=True) + EPS_UNIT)


def unit_back(values, grad):
    scale = unit_scale(values)
    along = jnp.sum(values * grad, axis=-1, keepdims=True)
    return grad * scale - values * (along * (scale * scale * scale))


def dot(left, right):
    return jnp.dot(left, right, preferred_element_type=F32)


def dot_last(left, right):
    return lax.dot_general(left, right, (((1,), (1,)), ((), ())), preferred_element_type=F32)


def dot_first(left, right):
    return lax.dot_general(left, right, (((0,), (0,)), ((), ())), preferred_element_type=F32)


def iota(shape, dim):
    return lax.broadcasted_iota(jnp.int32, shape, dim)


class Place:
    def __init__(self):
        self.me = lax.axis_index("dp")
        self.core = self.me % 2
        self.at = {"y": (self.me // 2) % 4, "z": (self.me // 8) % 4, "x": self.me // 32}
        self.partner = self.me + 1 - 2 * self.core

    def flip(self, kind, value):
        image, text = 3 - value, value + 1 - 2 * (value % 2)
        return image + kind * (text - image)

    def bit(self, kind, value):
        return value // 2 + kind * (value % 2 - value // 2)

    def coords(self, kind, offset):
        return {
            axis: self.flip(kind, self.at[axis]) if offset >> step & 1 else self.at[axis]
            for step, axis in enumerate("yzx")
        }

    def peer(self, kind, offset, core):
        where = self.coords(kind, offset)
        return ((where["x"] * 4 + where["z"]) * 4 + where["y"]) * 2 + core

    def slot(self, kind, offset):
        where = self.coords(kind, offset)
        bits = {axis: self.bit(kind, where[axis]) for axis in "yzx"}
        return bits["x"] * 4 + bits["z"] * 2 + bits["y"]


def kernel(
    captions,
    layout,
    images,
    w_query,
    w_keyval,
    w_out,
    w_up,
    w_down,
    w_proj,
    image_grad,
    text_grad,
    tokens,
    normed,
    end_rows,
    query_w,
    keyval_w,
    out_w,
    up_w,
    down_w,
    proj_w,
    attn_scores,
    attn,
    units,
    row_exp,
    col_exp,
    row_peak,
    col_peak,
    logs,
    row_log,
    blocks,
    parts,
    load_sem,
    weight_sem,
    gather_send,
    gather_recv,
    pass_send,
    pass_recv,
    log_send,
    log_recv,
    part_send,
    part_recv,
):
    place = Place()
    me, core, partner = place.me, place.core, place.partner
    other = 1 - core

    loads = []
    for step in range(LOAD_STEPS):
        span = pl.ds(step * STEP_T, STEP_T)
        copy = pltpu.make_async_copy(captions.at[span], tokens.at[span], load_sem.at[step])
        copy.start()
        loads.append(copy)
    weights = {}
    for number, (name, source, target) in enumerate(
        (
            ("query", w_query, query_w),
            ("keyval", w_keyval, keyval_w),
            ("out", w_out, out_w),
            ("up", w_up, up_w),
            ("down", w_down, down_w),
            ("proj", w_proj, proj_w),
        )
    ):
        weights[name] = pltpu.make_async_copy(source, target, weight_sem.at[number])
        weights[name].start()

    barrier = pltpu.get_barrier_semaphore()
    friends = [partner]
    for offset in range(1, CHIPS):
        for kind in range(2):
            friends += [place.peer(kind, offset, 0), place.peer(kind, offset, 1)]
    for friend in friends:
        pl.semaphore_signal(barrier, inc=1, device_id=(friend,), device_id_type=MESH)

    image_values = images[...].astype(F32)
    image_unit = (image_values * unit_scale(image_values)).astype(BF16)
    image_slot, text_slot = place.slot(0, 0), place.slot(1, 0)
    units[core, image_slot, 0] = image_unit

    span = pl.ds(pl.multiple_of(me // 4 * 128, 128), 128)
    counts = layout[0:1, span].astype(F32)
    picked = iota((CAPS, 128), 1) == iota((CAPS, 128), 0) + me % 4 * CAPS
    lengths = jnp.sum(jnp.where(picked, counts, 0.0), axis=1, keepdims=True)
    lengths = jnp.maximum(lengths, 1.0)

    end_rows[...] = jnp.zeros_like(end_rows)
    for step in range(LOAD_STEPS):
        loads[step].wait()

    def norm_step(step, _):
        for group in range(GROUPS):
            rows = slice(group * GROUP, (group + 1) * GROUP)
            ends = end_rows[rows, :]
            for inner in range(STEP_T):
                t = step * STEP_T + inner
                values = tokens[t, rows, :].astype(F32)
                at = pl.ds(pl.multiple_of(t * GROUP, GROUP), GROUP)
                normed[group, at, :] = norm_rows(values).astype(BF16)
                ends = jnp.where(lengths[rows] - 1.0 == t.astype(F32), values, ends)
            end_rows[rows, :] = ends
        return 0

    lax.fori_loop(0, LOAD_STEPS, norm_step, 0)

    end_values = end_rows[...]
    end_normed = norm_rows(end_values).astype(BF16)
    weights["query"].wait()
    query = dot(end_normed, query_w[...]).astype(BF16).astype(F32) * (1.0 / math.sqrt(HEAD_DIM))
    head_of = iota((GROUP, WIDTH), 1) // HEAD_DIM
    spread = jnp.concatenate(
        [
            jnp.where(head_of == head, query[group * GROUP : (group + 1) * GROUP], 0.0)
            for group in range(GROUPS)
            for head in range(HEADS)
        ],
        axis=0,
    ).astype(BF16)
    weights["keyval"].wait()
    key_query = dot_last(spread, keyval_w[:, :WIDTH]).astype(BF16)

    contexts = []
    same = iota((GROUP, COLS), 0) == iota((GROUP, COLS), 1) % GROUP
    for group in range(GROUPS):
        attn_scores[...] = dot_last(normed[group], key_query[group * COLS : (group + 1) * COLS])
        belongs = iota((CAPS, COLS), 0) == iota((CAPS, COLS), 1) % GROUP + group * GROUP
        limit = jnp.sum(jnp.where(belongs, lengths, 0.0), axis=0, keepdims=True)

        def at_token(t):
            return pl.ds(pl.multiple_of(t * GROUP, GROUP), GROUP)

        def peak_step(t, peak):
            inside = t.astype(F32) < limit
            return jnp.maximum(peak, jnp.where(inside, attn_scores[at_token(t), :], -jnp.inf))

        peak = lax.fori_loop(
            0, CTX, peak_step, jnp.full((GROUP, COLS), -jnp.inf, F32), unroll=STEP_T
        )

        def exp_step(t, total):
            inside = same & (t.astype(F32) < limit)
            value = jnp.where(inside, jnp.exp(attn_scores[at_token(t), :] - peak), 0.0)
            attn_scores[at_token(t), :] = value
            return total + value

        total = lax.fori_loop(0, CTX, exp_step, jnp.zeros((GROUP, COLS), F32), unroll=STEP_T)
        scale = jnp.where(same, 1.0 / jnp.where(same, total, 1.0), 0.0)

        def attn_step(t, _):
            attn[at_token(t), :] = (attn_scores[at_token(t), :] * scale).astype(BF16)
            return 0

        lax.fori_loop(0, CTX, attn_step, 0, unroll=STEP_T)
        contexts.append(dot_first(attn[...], normed[group]).astype(BF16))

    pl.semaphore_wait(barrier, len(friends))
    image_sends, text_sends = [], []
    for offset in range(CHIPS - 1, 0, -1):
        copy = pltpu.make_async_remote_copy(
            src_ref=units.at[core, image_slot, 0],
            dst_ref=units.at[core, image_slot, 0],
            send_sem=gather_send.at[0, offset],
            recv_sem=gather_recv.at[0, offset],
            device_id=(place.peer(0, offset, core),),
            device_id_type=MESH,
        )
        copy.start()
        image_sends.append((offset, copy))

    by_head = dot(jnp.concatenate(contexts, axis=0), keyval_w[:, WIDTH:])
    mixed = []
    for group in range(GROUPS):
        total = jnp.zeros((GROUP, WIDTH), F32)
        for head in range(HEADS):
            first = group * COLS + head * GROUP
            total = total + jnp.where(head_of == head, by_head[first : first + GROUP], 0.0)
        mixed.append(total)
    mixed = jnp.concatenate(mixed, axis=0).astype(BF16)

    weights["out"].wait()
    residual = (end_values + dot(mixed, out_w[...])).astype(BF16)
    residual = residual.astype(F32)
    inner = norm_rows(residual).astype(BF16)
    weights["up"].wait()
    weights["down"].wait()
    final = residual
    for part in range(FF // WIDTH):
        span = slice(part * WIDTH, (part + 1) * WIDTH)
        hidden = dot(inner, up_w[:, span])
        hidden = 0.5 * hidden * (1.0 + lax.erf(hidden * (1.0 / math.sqrt(2.0))))
        final = final + dot(hidden.astype(BF16), down_w[span, :])
    pooled = norm_rows(final).astype(BF16)
    weights["proj"].wait()
    text_values = dot(pooled, proj_w[...]).astype(BF16).astype(F32)
    text_unit = (text_values * unit_scale(text_values)).astype(BF16)
    units[other, text_slot, 0] = text_unit

    for offset in range(CHIPS - 1, 0, -1):
        copy = pltpu.make_async_remote_copy(
            src_ref=units.at[other, text_slot, 0],
            dst_ref=units.at[other, text_slot, 0],
            send_sem=gather_send.at[1, offset],
            recv_sem=gather_recv.at[1, offset],
            device_id=(place.peer(1, offset, core),),
            device_id_type=MESH,
        )
        copy.start()
        text_sends.append((offset, copy))

    def hand_on(kind, offset):
        mine, theirs = (core, other) if kind == 0 else (other, core)
        slot = place.slot(kind, offset)
        copy = pltpu.make_async_remote_copy(
            src_ref=units.at[mine, slot, 0],
            dst_ref=units.at[theirs, slot, 1],
            send_sem=pass_send.at[kind, offset],
            recv_sem=pass_recv.at[kind, offset],
            device_id=(partner,),
            device_id_type=MESH,
        )
        copy.start()
        return copy

    passed = [hand_on(1, 0), hand_on(0, 0)]
    for offset, copy in image_sends[::-1]:
        copy.wait_recv()
        passed.append(hand_on(0, offset))
    for offset, copy in text_sends[::-1]:
        copy.wait_recv()
        passed.append(hand_on(1, offset))
    for copy in passed:
        copy.wait_recv()

    others = units[1].reshape(ROWS, WIDTH)
    eye = iota((CHUNK, CHUNK), 0) == iota((CHUNK, CHUNK), 1)
    col_sums, col_peaks = [], []
    for chunk in range(CHUNKS):
        mine = units[0, 2 * chunk : 2 * chunk + 2].reshape(CHUNK, WIDTH)
        scores = LOGIT_SCALE * dot_last(mine, others)
        peak = jnp.max(scores, axis=1, keepdims=True)
        value = jnp.exp(scores - peak)
        row_exp[chunk] = value
        row_peak[chunk] = peak
        log = peak + jnp.log(jnp.sum(value, axis=1, keepdims=True))
        logs[0, 0, chunk : chunk + 1, :] = jnp.sum(
            jnp.where(eye, log, 0.0), axis=0, keepdims=True
        )
        peak = jnp.max(scores, axis=0, keepdims=True)
        value = jnp.exp(scores - peak)
        col_exp[chunk] = value
        col_peak[chunk] = peak
        col_peaks.append(peak)
        col_sums.append(jnp.sum(value, axis=0, keepdims=True))
    top = col_peaks[0]
    for peak in col_peaks[1:]:
        top = jnp.maximum(top, peak)
    total = sum(part * jnp.exp(peak - top) for part, peak in zip(col_sums, col_peaks))
    log = top + jnp.log(total)
    for chunk in range(CHUNKS):
        logs[1, 0, chunk : chunk + 1, :] = log[:, chunk * CHUNK : (chunk + 1) * CHUNK]

    log_sends = []
    for offset in range(CHIPS - 1, 0, -1):
        for side, kind in ((0, core), (1, other)):
            copy = pltpu.make_async_remote_copy(
                src_ref=logs.at[side, 0],
                dst_ref=logs.at[side, offset],
                send_sem=log_send.at[side, offset],
                recv_sem=log_recv.at[side, offset],
                device_id=(place.peer(kind, offset, core),),
                device_id_type=MESH,
            )
            copy.start()
            log_sends.append(copy)
    for copy in log_sends:
        copy.wait_recv()

    def whole_log(side):
        top = logs[side, 0]
        for offset in range(1, CHIPS):
            top = jnp.maximum(top, logs[side, offset])
        total = jnp.zeros_like(top)
        for offset in range(CHIPS):
            total = total + jnp.exp(logs[side, offset] - top)
        return top + jnp.log(total)

    row_logs, col_logs = whole_log(0), whole_log(1)
    for chunk in range(CHUNKS):
        row_log[chunk] = row_logs[chunk : chunk + 1, :]
    col_logs = jnp.concatenate([col_logs[chunk : chunk + 1, :] for chunk in range(CHUNKS)], axis=1)

    part_sends = []
    for pair in range(CHUNKS - 1, -1, -1):
        chunk = place.slot(core, 2 * pair) // 2
        log = jnp.sum(jnp.where(eye, row_log[chunk], 0.0), axis=1, keepdims=True)
        row_scale = jnp.exp(row_peak[chunk] - log)
        col_scale = jnp.exp(col_peak[chunk] - col_logs)
        weight = (row_exp[chunk] * row_scale + col_exp[chunk] * col_scale).astype(BF16)
        grad = dot(weight, others).astype(BF16).reshape(2, 2, CAPS, WIDTH)
        blocks[pl.ds(chunk * 2, 2)] = grad
        for offset in (2 * pair + 1, 2 * pair):
            slot = place.slot(core, offset)
            for side in range(2):
                if offset == 0 and side == 0:
                    parts[core, 0] = blocks[slot, 0]
                    continue
                copy = pltpu.make_async_remote_copy(
                    src_ref=blocks.at[slot, side],
                    dst_ref=parts.at[core, offset],
                    send_sem=part_send.at[offset, side],
                    recv_sem=part_recv.at[core, offset],
                    device_id=(place.peer(core, offset, core + side - 2 * side * core),),
                    device_id_type=MESH,
                )
                copy.start()
                part_sends.append(copy)

    def arrived(kind, offset):
        pltpu.make_async_remote_copy(
            src_ref=parts.at[kind, offset],
            dst_ref=parts.at[kind, offset],
            send_sem=part_send.at[0, 0],
            recv_sem=part_recv.at[kind, offset],
            device_id=(partner,),
            device_id_type=MESH,
        ).wait_recv()

    arrived(other, 0)
    for offset in range(1, CHIPS):
        for kind in range(2):
            arrived(kind, offset)

    half = 0.5 * LOGIT_SCALE
    sums = []
    for kind in range(2):
        total = parts[kind, 0].astype(F32)
        for offset in range(1, CHIPS):
            total = total + parts[kind, offset].astype(F32)
        sums.append(total)
    image_unit_grad = half * sums[0] - LOGIT_SCALE * text_unit.astype(F32)
    text_unit_grad = half * sums[1] - LOGIT_SCALE * image_unit.astype(F32)
    image_grad[...] = unit_back(image_values, image_unit_grad)
    text_grad[...] = unit_back(text_values, text_unit_grad)

    for _, copy in image_sends + text_sends:
        copy.wait_send()
    for copy in passed + log_sends + part_sends:
        copy.wait_send()


def body(captions, caption_layout, images, w_query, w_keyval, w_out, w_up, w_down, w_proj):
    hbm = pl.BlockSpec(memory_space=pl.ANY)
    vmem = pl.BlockSpec(memory_space=pltpu.VMEM)
    dma = pltpu.SemaphoreType.DMA
    return pl.pallas_call(
        kernel,
        out_shape=(
            jax.ShapeDtypeStruct((CAPS, WIDTH), F32),
            jax.ShapeDtypeStruct((CAPS, WIDTH), F32),
        ),
        in_specs=[hbm, vmem, vmem] + [hbm] * 6,
        out_specs=(vmem, vmem),
        scratch_shapes=[
            pltpu.VMEM((CTX, CAPS, WIDTH), BF16),
            pltpu.VMEM((GROUPS, TOKENS, WIDTH), BF16),
            pltpu.VMEM((CAPS, WIDTH), F32),
            pltpu.VMEM((WIDTH, WIDTH), BF16),
            pltpu.VMEM((WIDTH, 2 * WIDTH), BF16),
            pltpu.VMEM((WIDTH, WIDTH), BF16),
            pltpu.VMEM((WIDTH, FF), BF16),
            pltpu.VMEM((FF, WIDTH), BF16),
            pltpu.VMEM((WIDTH, WIDTH), BF16),
            pltpu.VMEM((TOKENS, COLS), F32),
            pltpu.VMEM((TOKENS, COLS), BF16),
            pltpu.VMEM((2, CHIPS, 2, CAPS, WIDTH), BF16),
            pltpu.VMEM((CHUNKS, CHUNK, ROWS), F32),
            pltpu.VMEM((CHUNKS, CHUNK, ROWS), F32),
            pltpu.VMEM((CHUNKS, CHUNK, 1), F32),
            pltpu.VMEM((CHUNKS, 1, ROWS), F32),
            pltpu.VMEM((2, CHIPS, CHUNKS, CHUNK), F32),
            pltpu.VMEM((CHUNKS, 1, CHUNK), F32),
            pltpu.VMEM((CHIPS, 2, CAPS, WIDTH), BF16),
            pltpu.VMEM((2, CHIPS, CAPS, WIDTH), BF16),
            dma((LOAD_STEPS,)),
            dma((6,)),
            dma((2, CHIPS)),
            dma((2, CHIPS)),
            dma((2, CHIPS)),
            dma((2, CHIPS)),
            dma((2, CHIPS)),
            dma((2, CHIPS)),
            dma((CHIPS, 2)),
            dma((2, CHIPS)),
        ],
        compiler_params=pltpu.CompilerParams(
            collective_id=0, has_side_effects=True, vmem_limit_bytes=60 * 1024 * 1024
        ),
    )(
        captions.transpose(1, 0, 2),
        caption_layout,
        images,
        w_query,
        w_keyval,
        w_out,
        w_up,
        w_down,
        w_proj,
    )


def solution(mesh):
    return jax.shard_map(
        body,
        mesh=mesh,
        in_specs=(P("dp", None, None), P(), P("dp", None), P(), P(), P(), P(), P(), P()),
        out_specs=(P("dp", None), P("dp", None)),
        check_vma=False,
    )
```

time: 235 us -> 53.6 us (0.23)
  waiting for transfers between devices: 76.8 us -> 0 us
  matrix products: 51.8 us -> 0 us
  Pallas kernels: 0 us -> 49.7 us
  local copies, waits for them, and re-layouts: 40.3 us -> 3.08 us
  blocking collectives: 35.6 us -> 0 us
  other arithmetic: 15 us -> 0 us
  between operations: 14.4 us -> 0.64 us
    all_gather x1 -> x0, waiting for transfers between devices: 76.8 us -> none  [body(): lax.all_gather(jnp.concatenate([image_unit, text_unit], axis=1), 'dp', ax...]
    dot_general x13 -> x0, matrix products: 51.8 us -> none  [the longest x2 9.66 us: contract_last(): lax.dot_general(left, right, (((1,), (1,)), ((), ())), preferred_element_...]
    pallas_call x0 -> x1, Pallas kernels: none -> 49.7 us  [body(): pl.pallas_call(kernel, out_shape=(jax.ShapeDtypeStruct((CAPS, WIDTH), F32...]
    all_gather x1 -> x0, blocking collectives: 35.6 us -> none  [turned_gather(): out, at, gathered = (lax.all_gather(both, axis, axis=0, tiled=True), 0, [])]
    slice x5 -> x0, local copies, waits for them, and re-layouts: 16.5 us -> none  [the longest x2 9.47 us: encode(): key_heads = keyval[:, :model_width].reshape(total_rows, HEADS, head_dim)]
    gather x2 -> x0, local copies, waits for them, and re-layouts: 7.79 us -> none  [the longest x1 3.95 us: encode(): normed[last_row]]
    reshape x3 -> x0, local copies, waits for them, and re-layouts: 6.05 us -> none  [the longest x1 4.98 us: body(): token_rows = captions.reshape(-1, model_width)]
    unnamed x40 -> x2, local copies, waits for them, and re-layouts: 8.83 us -> 3.08 us
  transfers between devices with their start and end apart: 1 -> 0, of which waited for: 1 -> 0; matrix products, arithmetic and copies ran while one was open for 0% -> 0% of each run, Pallas kernels for 0% -> 0%
where the time goes in v1:
time: 53.6 us; the launch traced here: 53.4 us
  Pallas kernels  49.7 us (93%)
  local copies, waits for them, and re-layouts  3.08 us (6%)
  between operations  0.64 us (1%)
    pallas_call x1, Pallas kernels, body(): pl.pallas_call(kernel, out_shape=(jax.ShapeDtypeStruct((CAPS, WIDTH), F32...  49.7 us
    unnamed x2, local copies, waits for them, and re-layouts  3.08 us

profile of v1, /device:TPU:1, one launch (start us, length us, event | category | flops | bytes accessed | tf_op | source)
XLA Modules:
  0.0 53.4 jit_solution(12112814639954708015)
XLA Ops:
  0.6 49.7 %shard_map.104 = (f32[32,768]{1,0:T(8,128)}, f32[32,768]{1,0:T(8,128)}) custom-call(bf16[77,32,768]{2,1,0:T(8,128)(2,1)} %bitcast.1, s32[2,4096]{1,0:T(2,128)} %layout.1, bf16[32,768]{1,0:T(8,128)(2,1)} %images.1, bf16[768,768]{1,0:T(8,128)(2,1)} %w_query.1, bf16[768,1536]{1,0:T(8,128)(2,1)} %w_keyval.1, bf16[768,768]{1,0:T(8,128)(2,1)} %w_out.1, ...), custom_call_target="tpu_custom_call" | custom-call | tf_op jit(solution)/shard_map/pallas_call | solution.py:452
  50.3 1.5 %copy.13 = f32[32,768]{1,0:T(8,128)} copy(f32[32,768]{1,0:T(8,128)} %get-tuple-element.4) | data formatting | bytes 196608
  51.9 1.5 %copy.14 = f32[32,768]{1,0:T(8,128)} copy(f32[32,768]{1,0:T(8,128)} %get-tuple-element.5) | data formatting | bytes 196608

commit v2 on v1

--- a/solution.py
+++ b/solution.py
@@ -27,6 +27,7 @@
 LOGIT_SCALE = 100.0
 EPS_NORM = 1e-05
 EPS_UNIT = 1e-06
+LOG2_E = math.log2(math.e)
 
 MESH = pl.DeviceIdType.MESH
 F32 = jnp.float32
@@ -142,12 +143,12 @@
     me, core, partner = place.me, place.core, place.partner
     other = 1 - core
 
-    loads = []
+    def load(step):
+        span = pl.ds(step * STEP_T, STEP_T)
+        return pltpu.make_async_copy(captions.at[span], tokens.at[span], load_sem.at[step])
+
     for step in range(LOAD_STEPS):
-        span = pl.ds(step * STEP_T, STEP_T)
-        copy = pltpu.make_async_copy(captions.at[span], tokens.at[span], load_sem.at[step])
-        copy.start()
-        loads.append(copy)
+        load(step).start()
     weights = {}
     for number, (name, source, target) in enumerate(
         (
@@ -160,7 +161,7 @@
         )
     ):
         weights[name] = pltpu.make_async_copy(source, target, weight_sem.at[number])
-        weights[name].start()
+    weights["query"].start()
 
     barrier = pltpu.get_barrier_semaphore()
     friends = [partner]
@@ -182,10 +183,19 @@
     lengths = jnp.maximum(lengths, 1.0)
 
     end_rows[...] = jnp.zeros_like(end_rows)
-    for step in range(LOAD_STEPS):
-        loads[step].wait()
 
     def norm_step(step, _):
+        load(step).wait()
+
+        @pl.when(step == 1)
+        def _():
+            weights["keyval"].start()
+
+        @pl.when(step == 3)
+        def _():
+            for name in ("out", "up", "down", "proj"):
+                weights[name].start()
+
         for group in range(GROUPS):
             rows = slice(group * GROUP, (group + 1) * GROUP)
             ends = end_rows[rows, :]
@@ -199,6 +209,20 @@
         return 0
 
     lax.fori_loop(0, LOAD_STEPS, norm_step, 0)
+
+    pl.semaphore_wait(barrier, len(friends))
+    image_sends, text_sends = [], []
+    for offset in range(CHIPS - 1, 0, -1):
+        copy = pltpu.make_async_remote_copy(
+            src_ref=units.at[core, image_slot, 0],
+            dst_ref=units.at[core, image_slot, 0],
+            send_sem=gather_send.at[0, offset],
+            recv_sem=gather_recv.at[0, offset],
+            device_id=(place.peer(0, offset, core),),
+            device_id_type=MESH,
+        )
+        copy.start()
+        image_sends.append((offset, copy))
 
     end_values = end_rows[...]
     end_normed = norm_rows(end_values).astype(BF16)
@@ -214,9 +238,10 @@
         axis=0,
     ).astype(BF16)
     weights["keyval"].wait()
-    key_query = dot_last(spread, keyval_w[:, :WIDTH]).astype(BF16)
+    key_query = (dot_last(spread, keyval_w[:, :WIDTH]) * LOG2_E).astype(BF16)
 
     contexts = []
+    turn = iota((COLS, COLS), 0) == iota((COLS, COLS), 1)
     same = iota((GROUP, COLS), 0) == iota((GROUP, COLS), 1) % GROUP
     for group in range(GROUPS):
         attn_scores[...] = dot_last(normed[group], key_query[group * COLS : (group + 1) * COLS])
@@ -231,38 +256,22 @@
             return jnp.maximum(peak, jnp.where(inside, attn_scores[at_token(t), :], -jnp.inf))
 
         peak = lax.fori_loop(
-            0, CTX, peak_step, jnp.full((GROUP, COLS), -jnp.inf, F32), unroll=STEP_T
+            0, CTX, peak_step, jnp.full((GROUP, COLS), -jnp.inf, F32), unroll=CTX
         )
 
+        peak = jnp.where(same, peak, jnp.inf)
+
         def exp_step(t, total):
-            inside = same & (t.astype(F32) < limit)
-            value = jnp.where(inside, jnp.exp(attn_scores[at_token(t), :] - peak), 0.0)
-            attn_scores[at_token(t), :] = value
+            inside = t.astype(F32) < limit
+            value = jnp.where(inside, attn_scores[at_token(t), :], -jnp.inf)
+            value = jnp.exp2(value - peak)
+            attn[at_token(t), :] = value.astype(BF16)
             return total + value
 
-        total = lax.fori_loop(0, CTX, exp_step, jnp.zeros((GROUP, COLS), F32), unroll=STEP_T)
-        scale = jnp.where(same, 1.0 / jnp.where(same, total, 1.0), 0.0)
-
-        def attn_step(t, _):
-            attn[at_token(t), :] = (attn_scores[at_token(t), :] * scale).astype(BF16)
-            return 0
-
-        lax.fori_loop(0, CTX, attn_step, 0, unroll=STEP_T)
-        contexts.append(dot_first(attn[...], normed[group]).astype(BF16))
-
-    pl.semaphore_wait(barrier, len(friends))
-    image_sends, text_sends = [], []
-    for offset in range(CHIPS - 1, 0, -1):
-        copy = pltpu.make_async_remote_copy(
-            src_ref=units.at[core, image_slot, 0],
-            dst_ref=units.at[core, image_slot, 0],
-            send_sem=gather_send.at[0, offset],
-            recv_sem=gather_recv.at[0, offset],
-            device_id=(place.peer(0, offset, core),),
-            device_id_type=MESH,
-        )
-        copy.start()
-        image_sends.append((offset, copy))
+        total = lax.fori_loop(0, CTX, exp_step, jnp.zeros((GROUP, COLS), F32), unroll=CTX)
+        total = jnp.sum(total, axis=0, keepdims=True)
+        total = jnp.sum(jnp.where(turn, total, 0.0), axis=1, keepdims=True)
+        contexts.append((dot_first(attn[...], normed[group]) / total).astype(BF16))
 
     by_head = dot(jnp.concatenate(contexts, axis=0), keyval_w[:, WIDTH:])
     mixed = []
@@ -445,16 +454,19 @@
         copy.wait_send()
 
 
+def hand_out(image_from, text_from, image_to, text_to):
+    image_to[...] = image_from[...]
+    text_to[...] = text_from[...]
+
+
 def body(captions, caption_layout, images, w_query, w_keyval, w_out, w_up, w_down, w_proj):
     hbm = pl.BlockSpec(memory_space=pl.ANY)
     vmem = pl.BlockSpec(memory_space=pltpu.VMEM)
     dma = pltpu.SemaphoreType.DMA
-    return pl.pallas_call(
+    grads = (jax.ShapeDtypeStruct((CAPS, WIDTH), F32),) * 2
+    made = pl.pallas_call(
         kernel,
-        out_shape=(
-            jax.ShapeDtypeStruct((CAPS, WIDTH), F32),
-            jax.ShapeDtypeStruct((CAPS, WIDTH), F32),
-        ),
+        out_shape=grads,
         in_specs=[hbm, vmem, vmem] + [hbm] * 6,
         out_specs=(vmem, vmem),
         scratch_shapes=[
@@ -503,6 +515,7 @@
         w_down,
         w_proj,
     )
+    return pl.pallas_call(hand_out, out_shape=grads, in_specs=[vmem] * 2, out_specs=(vmem, vmem))(*made)
 
 
 def solution(mesh):

time: 53.6 us -> 45 us (0.84)
  Pallas kernels: 49.7 us -> 44.2 us
  local copies, waits for them, and re-layouts: 3.08 us -> 0 us
    pallas_call x1 -> x2, Pallas kernels: 49.7 us -> 44.2 us  [the longest x1 42.6 us: body(): pl.pallas_call(kernel, out_shape=grads, in_specs=[hbm, vmem, vmem] + [hbm...]
    unnamed x2 -> x0, local copies, waits for them, and re-layouts: 3.08 us -> none
where the time goes in v2:
time: 45 us; the launch traced here: 44.8 us
  Pallas kernels  44.2 us (98%)
  between operations  0.64 us (1%)
    pallas_call x1, Pallas kernels, body(): pl.pallas_call(kernel, out_shape=grads, in_specs=[hbm, vmem, vmem] + [hbm...  42.6 us
    pallas_call x1, Pallas kernels, body(): pl.pallas_call(hand_out, out_shape=grads, in_specs=[vmem] * 2, out_specs=...  1.62 us

profile of v2, /device:TPU:1, one launch (start us, length us, event | category | flops | bytes accessed | tf_op | source)
XLA Modules:
  0.0 44.8 jit_solution(11734734244679139466)
XLA Ops:
  0.6 42.6 %shard_map.104 = (f32[32,768]{1,0:T(8,128)}, f32[32,768]{1,0:T(8,128)}) custom-call(bf16[77,32,768]{2,1,0:T(8,128)(2,1)} %bitcast.1, s32[2,4096]{1,0:T(2,128)} %layout.1, bf16[32,768]{1,0:T(8,128)(2,1)} %images.1, bf16[768,768]{1,0:T(8,128)(2,1)} %w_query.1, bf16[768,1536]{1,0:T(8,128)(2,1)} %w_keyval.1, bf16[768,768]{1,0:T(8,128)(2,1)} %w_out.1, ...), custom_call_target="tpu_custom_call" | custom-call | tf_op jit(solution)/shard_map/pallas_call | solution.py:467
  43.2 1.6 %shard_map.105 = (f32[32,768]{1,0:T(8,128)}, f32[32,768]{1,0:T(8,128)}) custom-call(f32[32,768]{1,0:T(8,128)} %get-tuple-element.4.image_from, f32[32,768]{1,0:T(8,128)} %get-tuple-element.5.text_from), custom_call_target="tpu_custom_call" | custom-call | tf_op jit(solution)/shard_map/pallas_call | solution.py:518

commit v3 on v2

v3 whole, which is shorter than its diff:
```python
import math

import jax
import jax.numpy as jnp
from jax import lax
from jax.experimental import pallas as pl
from jax.experimental.pallas import tpu as pltpu
from jax.sharding import PartitionSpec as P

HEADS = 12
HEAD_DIM = 64
WIDTH = 768
CTX = 77
CAPS = 32
FF = 3072
GROUP = 16
GROUPS = CAPS // GROUP
SPLIT = HEADS * GROUP
TOKENS = CTX * GROUP
TOKENS_PAD = -(-TOKENS // 256) * 256
BLOCK = 256
BLOCK_HEADS = BLOCK // HEAD_DIM
LOAD_STEPS = 7
STEP_T = CTX // LOAD_STEPS
NORM_UNROLL = 11
CHIPS = 8
ROWS = CHIPS * 2 * CAPS
HALF = ROWS // 2
PIECE = 128
PIECES = ROWS // PIECE

LOGIT_SCALE = 100.0
EPS_NORM = 1e-05
EPS_UNIT = 1e-06
LOG2_E = math.log2(math.e)

MESH = pl.DeviceIdType.MESH
F32 = jnp.float32
BF16 = jnp.bfloat16


def norm_rows(values):
    center = values - jnp.mean(values, axis=-1, keepdims=True)
    spread = jnp.mean(center * center, axis=-1, keepdims=True)
    return center * lax.rsqrt(spread + EPS_NORM)


def unit_scale(values):
    return lax.rsqrt(jnp.sum(values * values, axis=-1, keepdims=True) + EPS_UNIT)


def unit_back(values, grad):
    scale = unit_scale(values)
    along = jnp.sum(values * grad, axis=-1, keepdims=True)
    return grad * scale - values * (along * (scale * scale * scale))


def dot(left, right):
    return jnp.dot(left, right, preferred_element_type=F32)


def dot_last(left, right):
    return lax.dot_general(left, right, (((1,), (1,)), ((), ())), preferred_element_type=F32)


def dot_first(left, right):
    return lax.dot_general(left, right, (((0,), (0,)), ((), ())), preferred_element_type=F32)


def iota(shape, dim):
    return lax.broadcasted_iota(jnp.int32, shape, dim)


class Place:
    def __init__(self):
        self.me = lax.axis_index("dp")
        self.core = self.me % 2
        self.at = {"y": (self.me // 2) % 4, "z": (self.me // 8) % 4, "x": self.me // 32}
        self.partner = self.me + 1 - 2 * self.core

    def flip(self, kind, value):
        image, text = 3 - value, value + 1 - 2 * (value % 2)
        return image + kind * (text - image)

    def bit(self, kind, value):
        return value // 2 + kind * (value % 2 - value // 2)

    def coords(self, kind, offset):
        return {
            axis: self.flip(kind, self.at[axis]) if offset >> step & 1 else self.at[axis]
            for step, axis in enumerate("yzx")
        }

    def peer(self, kind, offset, core):
        where = self.coords(kind, offset)
        return ((where["x"] * 4 + where["z"]) * 4 + where["y"]) * 2 + core

    def slot(self, kind, offset):
        where = self.coords(kind, offset)
        bits = {axis: self.bit(kind, where[axis]) for axis in "yzx"}
        return bits["x"] * 4 + bits["z"] * 2 + bits["y"]


def kernel(
    captions,
    layout,
    images,
    w_query,
    w_keyval,
    w_out,
    w_up,
    w_down,
    w_proj,
    image_grad,
    text_grad,
    tokens,
    normed,
    query_w,
    keyval_w,
    out_w,
    up_w,
    down_w,
    proj_w,
    counts,
    ends,
    image_rows,
    attn_scores,
    attn_bias,
    attn,
    units,
    row_exp,
    col_exp,
    row_peak,
    col_peak,
    logs,
    weight,
    blocks,
    parts,
    small_sem,
    load_sem,
    weight_sem,
    gather_send,
    gather_recv,
    pass_send,
    pass_recv,
    log_send,
    log_recv,
    part_send,
    part_recv,
):
    place = Place()
    me, core, partner = place.me, place.core, place.partner
    other = 1 - core

    def load(step):
        span = pl.ds(step * STEP_T, STEP_T)
        return pltpu.make_async_copy(captions.at[span], tokens.at[span], load_sem.at[step])

    span = pl.ds(pl.multiple_of(me // 4 * 128, 128), 128)
    load_counts = pltpu.make_async_copy(layout.at[:, span], counts, small_sem.at[0])
    load_images = pltpu.make_async_copy(images, image_rows, small_sem.at[1])
    load_ends = pltpu.make_async_copy(layout.at[:, span], ends, small_sem.at[2])
    for step in range(LOAD_STEPS):
        load(step).start()
    for copy in (load_counts, load_ends, load_images):
        copy.start()
    weights = {}
    for number, (name, source, target) in enumerate(
        (
            ("query", w_query, query_w),
            ("keyval", w_keyval, keyval_w),
            ("out", w_out, out_w),
            ("up", w_up, up_w),
            ("down", w_down, down_w),
            ("proj", w_proj, proj_w),
        )
    ):
        weights[name] = pltpu.make_async_copy(source, target, weight_sem.at[number])
    weights["query"].start()

    barrier = pltpu.get_barrier_semaphore()
    friends = [partner]
    for offset in range(1, CHIPS):
        for kind in range(2):
            friends += [place.peer(kind, offset, 0), place.peer(kind, offset, 1)]
    for friend in friends:
        pl.semaphore_signal(barrier, inc=1, device_id=(friend,), device_id_type=MESH)

    normed[:, TOKENS:, :] = jnp.zeros((GROUPS, TOKENS_PAD - TOKENS, WIDTH), BF16)

    def norm_step(step, _):
        load(step).wait()

        @pl.when(step == 1)
        def _():
            weights["keyval"].start()

        @pl.when(step == 3)
        def _():
            for name in ("out", "up", "down", "proj"):
                weights[name].start()

        def token_step(inner, _):
            t = step * STEP_T + inner
            at = pl.ds(pl.multiple_of(t * GROUP, GROUP), GROUP)
            for group in range(GROUPS):
                rows = slice(group * GROUP, (group + 1) * GROUP)
                values = tokens[t, rows, :].astype(F32)
                normed[group, at, :] = norm_rows(values).astype(BF16)
            return 0

        return lax.fori_loop(0, STEP_T, token_step, 0, unroll=NORM_UNROLL)

    lax.fori_loop(0, LOAD_STEPS, norm_step, 0)

    load_images.wait()
    image_values = image_rows[...].astype(F32)
    image_unit = (image_values * unit_scale(image_values)).astype(BF16)
    slots = (place.slot(0, 0), place.slot(1, 0))
    units[0, 0, slots[0]] = image_unit

    pl.semaphore_wait(barrier, len(friends))

    def send_units(kind):
        copies = {}
        for offset in range(CHIPS - 1, 0, -1):
            copies[offset] = pltpu.make_async_remote_copy(
                src_ref=units.at[kind, 0, slots[kind]],
                dst_ref=units.at[kind, 0, slots[kind]],
                send_sem=gather_send.at[kind, offset],
                recv_sem=gather_recv.at[kind, offset],
                device_id=(place.peer(kind, offset, core),),
                device_id_type=MESH,
            )
            copies[offset].start()
        return copies

    def hand_on(kind, offset):
        slot = place.slot(kind, offset)
        copy = pltpu.make_async_remote_copy(
            src_ref=units.at[kind, 0, slot],
            dst_ref=units.at[kind, 1, slot],
            send_sem=pass_send.at[kind, offset],
            recv_sem=pass_recv.at[kind, offset],
            device_id=(partner,),
            device_id_type=MESH,
        )
        copy.start()
        return copy

    image_sends = send_units(0)
    passed = {(0, 0): hand_on(0, 0)}

    load_counts.wait()
    picked = iota((CAPS, 128), 1) == iota((CAPS, 128), 0) + me % 4 * CAPS
    lengths = jnp.sum(jnp.where(picked, counts[0:1, :].astype(F32), 0.0), axis=1, keepdims=True)
    lengths = jnp.maximum(lengths, 1.0)

    token = iota((GROUP, TOKENS_PAD), 1)
    own = token % GROUP == iota((GROUP, TOKENS_PAD), 0)
    for group in range(GROUPS):
        count = lengths[group * GROUP : (group + 1) * GROUP]
        inside = own & ((token // GROUP).astype(F32) < count)
        attn_bias[group] = jnp.where(inside, 0.0, -jnp.inf)

    load_ends.wait()
    end_values = []
    for group in range(GROUPS):
        rows = jnp.zeros((GROUP, WIDTH), BF16)
        for inner in range(GROUP):
            caption = group * GROUP + inner
            last = jnp.clip(ends[0, me % 4 * CAPS + caption] - 1, 0, CTX - 1)
            found = tokens[last, group * GROUP : (group + 1) * GROUP, :]
            rows = jnp.where(iota((GROUP, WIDTH), 0) == inner, found, rows)
        end_values.append(rows)
    end_values = jnp.concatenate(end_values, axis=0).astype(F32)
    end_normed = norm_rows(end_values).astype(BF16)
    weights["query"].wait()
    query = dot(end_normed, query_w[...]).astype(BF16).astype(F32) * (1.0 / math.sqrt(HEAD_DIM))
    head_of = iota((GROUP, BLOCK), 1) // HEAD_DIM
    groups = [slice(group * GROUP, (group + 1) * GROUP) for group in range(GROUPS)]
    spans = [slice(at, at + BLOCK) for at in range(0, WIDTH, BLOCK)]
    weights["keyval"].wait()
    key_query = []
    for span in spans:
        spread = [
            jnp.where(head_of == head, query[rows, span], 0.0)
            for rows in groups
            for head in range(BLOCK_HEADS)
        ]
        spread = jnp.concatenate(spread, axis=0).astype(BF16)
        key_query.append((dot_last(spread, keyval_w[:, span]) * LOG2_E).astype(BF16))

    part = BLOCK_HEADS * GROUP
    contexts = []
    for group in range(GROUPS):
        rows = slice(group * part, (group + 1) * part)
        asked = jnp.concatenate([block[rows] for block in key_query], axis=0)
        attn_scores[...] = dot_last(asked, normed[group])
        totals = []
        for head in range(HEADS):
            rows = slice(head * GROUP, (head + 1) * GROUP)
            value = attn_scores[rows, :] + attn_bias[group]
            value = jnp.exp2(value - jnp.max(value, axis=1, keepdims=True))
            attn[rows, :] = value.astype(BF16)
            totals.append(jnp.sum(value, axis=1, keepdims=True))
        context = dot(attn[...], normed[group]) / jnp.concatenate(totals, axis=0)
        contexts.append(context.astype(BF16))

    mixed = []
    for number, span in enumerate(spans):
        rows = slice(number * part, (number + 1) * part)
        by_head = jnp.concatenate([context[rows] for context in contexts], axis=0)
        by_head = dot(by_head, keyval_w[:, WIDTH + span.start : WIDTH + span.stop])
        sums = []
        for group in range(GROUPS):
            total = jnp.zeros((GROUP, BLOCK), F32)
            for head in range(BLOCK_HEADS):
                first = group * part + head * GROUP
                total = total + jnp.where(head_of == head, by_head[first : first + GROUP], 0.0)
            sums.append(total)
        mixed.append(jnp.concatenate(sums, axis=0))
    mixed = jnp.concatenate(mixed, axis=1).astype(BF16)

    weights["out"].wait()
    residual = (end_values + dot(mixed, out_w[...])).astype(BF16)
    residual = residual.astype(F32)
    inner = norm_rows(residual).astype(BF16)
    weights["up"].wait()
    weights["down"].wait()
    final = residual
    for part in range(FF // WIDTH):
        span = slice(part * WIDTH, (part + 1) * WIDTH)
        hidden = dot(inner, up_w[:, span])
        hidden = 0.5 * hidden * (1.0 + lax.erf(hidden * (1.0 / math.sqrt(2.0))))
        final = final + dot(hidden.astype(BF16), down_w[span, :])
    pooled = norm_rows(final).astype(BF16)
    weights["proj"].wait()
    text_values = dot(pooled, proj_w[...]).astype(BF16).astype(F32)
    text_unit = (text_values * unit_scale(text_values)).astype(BF16)
    units[1, 0, slots[1]] = text_unit

    text_sends = send_units(1)
    passed[1, 0] = hand_on(1, 0)

    for offset in range(1, CHIPS):
        image_sends[offset].wait_recv()
        passed[0, offset] = hand_on(0, offset)

    for offset in range(CHIPS - 1, 0, -1):
        text_sends[offset].wait_recv()
        passed[1, offset] = hand_on(1, offset)
    for offset in range(CHIPS):
        passed[0, offset].wait_recv()

    eye = iota((PIECE, PIECE), 0) == iota((PIECE, PIECE), 1)
    col_sums, col_peaks = [], []
    for half in range(2):
        if half == 1:
            for offset in range(CHIPS):
                passed[1, offset].wait_recv()
        scores = dot_last(units[1, half].reshape(HALF, WIDTH), units[0].reshape(ROWS, WIDTH))
        scores = scores * (LOGIT_SCALE * LOG2_E)
        peak = jnp.max(scores, axis=1, keepdims=True)
        value = jnp.exp2(scores - peak)
        row_exp[half] = value
        row_peak[half] = peak
        log = peak + jnp.log(jnp.sum(value, axis=1, keepdims=True)) * LOG2_E
        for piece in range(HALF // PIECE):
            part = log[piece * PIECE : (piece + 1) * PIECE]
            part = jnp.sum(jnp.where(eye, part, 0.0), axis=0, keepdims=True)
            logs[1, 0, half * (HALF // PIECE) + piece] = part
        peak = jnp.max(scores, axis=0, keepdims=True)
        value = jnp.exp2(scores - peak)
        col_exp[half] = value
        col_peak[half] = peak
        col_peaks.append(peak)
        col_sums.append(jnp.sum(value, axis=0, keepdims=True))
    top = jnp.maximum(*col_peaks)
    total = sum(part * jnp.exp2(peak - top) for part, peak in zip(col_sums, col_peaks))
    log = top + jnp.log(total) * LOG2_E
    for piece in range(PIECES):
        logs[0, 0, piece] = log[:, piece * PIECE : (piece + 1) * PIECE]

    log_sends = []
    for offset in range(CHIPS - 1, 0, -1):
        for kind in range(2):
            copy = pltpu.make_async_remote_copy(
                src_ref=logs.at[kind, 0],
                dst_ref=logs.at[kind, offset],
                send_sem=log_send.at[kind, offset],
                recv_sem=log_recv.at[kind, offset],
                device_id=(place.peer(kind, offset, core),),
                device_id_type=MESH,
            )
            copy.start()
            log_sends.append(copy)
    for copy in log_sends:
        copy.wait_recv()

    def whole_log(kind):
        top = logs[kind, 0]
        for offset in range(1, CHIPS):
            top = jnp.maximum(top, logs[kind, offset])
        total = jnp.zeros_like(top)
        for offset in range(CHIPS):
            total = total + jnp.exp2(logs[kind, offset] - top)
        return top + jnp.log(total) * LOG2_E

    image_logs, text_logs = whole_log(0), whole_log(1)
    image_logs = jnp.concatenate([image_logs[piece] for piece in range(PIECES)], axis=1)
    for half in range(2):
        col_scale = jnp.exp2(col_peak[half] - image_logs)
        for piece in range(HALF // PIECE):
            rows = slice(piece * PIECE, (piece + 1) * PIECE)
            first = half * HALF + piece * PIECE
            log = text_logs[half * (HALF // PIECE) + piece]
            log = jnp.sum(jnp.where(eye, log, 0.0), axis=1, keepdims=True)
            row_scale = jnp.exp2(row_peak[half, rows] - log)
            both = row_exp[half, rows] * row_scale + col_exp[half, rows] * col_scale
            weight[first : first + PIECE, :] = both.astype(BF16)

    part_sends = []
    for far in (1, 0):
        for side in range(2):
            first = place.slot(core, 4 * far) // 4 * 4
            span = pl.ds(pl.multiple_of(side * HALF + first * CAPS, PIECE), PIECE)

            def keep(grad):
                blocks[side, pl.ds(first, 4)] = grad.astype(BF16).reshape(4, CAPS, WIDTH)

            @pl.when(core == 0)
            def _():
                keep(dot_first(weight[:, span], units[1].reshape(ROWS, WIDTH)))

            @pl.when(core == 1)
            def _():
                keep(dot(weight[span, :], units[0].reshape(ROWS, WIDTH)))

            for offset in range(4 * far + 3, 4 * far - 1, -1):
                slot = place.slot(core, offset)
                if offset == 0 and side == 0:
                    parts[core, 0] = blocks[0, slot]
                    continue
                copy = pltpu.make_async_remote_copy(
                    src_ref=blocks.at[side, slot],
                    dst_ref=parts.at[core, offset],
                    send_sem=part_send.at[offset, side],
                    recv_sem=part_recv.at[core, offset],
                    device_id=(place.peer(core, offset, core + side - 2 * side * core),),
                    device_id_type=MESH,
                )
                copy.start()
                part_sends.append(copy)

    def arrived(kind, offset):
        pltpu.make_async_remote_copy(
            src_ref=parts.at[kind, offset],
            dst_ref=parts.at[kind, offset],
            send_sem=part_send.at[0, 0],
            recv_sem=part_recv.at[kind, offset],
            device_id=(partner,),
            device_id_type=MESH,
        ).wait_recv()

    arrived(other, 0)
    for offset in range(1, CHIPS):
        for kind in range(2):
            arrived(kind, offset)

    half = 0.5 * LOGIT_SCALE
    sums = []
    for kind in range(2):
        total = parts[kind, 0].astype(F32)
        for offset in range(1, CHIPS):
            total = total + parts[kind, offset].astype(F32)
        sums.append(total)
    image_unit_grad = half * sums[0] - LOGIT_SCALE * text_unit.astype(F32)
    text_unit_grad = half * sums[1] - LOGIT_SCALE * image_unit.astype(F32)
    image_grad[...] = unit_back(image_values, image_unit_grad)
    text_grad[...] = unit_back(text_values, text_unit_grad)

    for copy in [*image_sends.values(), *text_sends.values(), *passed.values()]:
        copy.wait_send()
    for copy in log_sends + part_sends:
        copy.wait_send()


def hand_out(image_from, text_from, image_to, text_to):
    image_to[...] = image_from[...]
    text_to[...] = text_from[...]


def body(captions, caption_layout, images, w_query, w_keyval, w_out, w_up, w_down, w_proj):
    hbm = pl.BlockSpec(memory_space=pl.ANY)
    vmem = pl.BlockSpec(memory_space=pltpu.VMEM)
    dma = pltpu.SemaphoreType.DMA
    grads = (jax.ShapeDtypeStruct((CAPS, WIDTH), F32),) * 2
    made = pl.pallas_call(
        kernel,
        out_shape=grads,
        in_specs=[hbm] * 9,
        out_specs=(vmem, vmem),
        scratch_shapes=[
            pltpu.VMEM((CTX, CAPS, WIDTH), BF16),
            pltpu.VMEM((GROUPS, TOKENS_PAD, WIDTH), BF16),
            pltpu.VMEM((WIDTH, WIDTH), BF16),
            pltpu.VMEM((WIDTH, 2 * WIDTH), BF16),
            pltpu.VMEM((WIDTH, WIDTH), BF16),
            pltpu.VMEM((WIDTH, FF), BF16),
            pltpu.VMEM((FF, WIDTH), BF16),
            pltpu.VMEM((WIDTH, WIDTH), BF16),
            pltpu.VMEM((2, 128), jnp.int32),
            pltpu.SMEM((2, 128), jnp.int32),
            pltpu.VMEM((CAPS, WIDTH), BF16),
            pltpu.VMEM((SPLIT, TOKENS_PAD), F32),
            pltpu.VMEM((GROUPS, GROUP, TOKENS_PAD), F32),
            pltpu.VMEM((SPLIT, TOKENS_PAD), BF16),
            pltpu.VMEM((2, 2, CHIPS, CAPS, WIDTH), BF16),
            pltpu.VMEM((2, HALF, ROWS), F32),
            pltpu.VMEM((2, HALF, ROWS), F32),
            pltpu.VMEM((2, HALF, 1), F32),
            pltpu.VMEM((2, 1, ROWS), F32),
            pltpu.VMEM((2, CHIPS, PIECES, 1, PIECE), F32),
            pltpu.VMEM((ROWS, ROWS), BF16),
            pltpu.VMEM((2, CHIPS, CAPS, WIDTH), BF16),
            pltpu.VMEM((2, CHIPS, CAPS, WIDTH), BF16),
            dma((3,)),
            dma((LOAD_STEPS,)),
            dma((6,)),
            dma((2, CHIPS)),
            dma((2, CHIPS)),
            dma((2, CHIPS)),
            dma((2, CHIPS)),
            dma((2, CHIPS)),
            dma((2, CHIPS)),
            dma((CHIPS, 2)),
            dma((2, CHIPS)),
        ],
        compiler_params=pltpu.CompilerParams(
            collective_id=0, has_side_effects=True, vmem_limit_bytes=60 * 1024 * 1024
        ),
    )(
        captions.transpose(1, 0, 2),
        caption_layout,
        images,
        w_query,
        w_keyval,
        w_out,
        w_up,
        w_down,
        w_proj,
    )
    return pl.pallas_call(hand_out, out_shape=grads, in_specs=[vmem] * 2, out_specs=(vmem, vmem))(*made)


def solution(mesh):
    return jax.shard_map(
        body,
        mesh=mesh,
        in_specs=(P("dp", None, None), P(), P("dp", None), P(), P(), P(), P(), P(), P()),
        out_specs=(P("dp", None), P("dp", None)),
        check_vma=False,
    )
```

time: 45 us -> 42.3 us (0.940)
  Pallas kernels: 44.2 us -> 41.5 us
    pallas_call x1, Pallas kernels: 42.6 us -> 39.9 us  [body(): pl.pallas_call(kernel, out_shape=grads, in_specs=[hbm] * 9, out_specs=(vm...]
where the time goes in v3:
time: 42.3 us; the launch traced here: 42.1 us
  Pallas kernels  41.5 us (98%)
  between operations  0.64 us (2%)
    pallas_call x1, Pallas kernels, body(): pl.pallas_call(kernel, out_shape=grads, in_specs=[hbm] * 9, out_specs=(vm...  39.9 us
    pallas_call x1, Pallas kernels, body(): pl.pallas_call(hand_out, out_shape=grads, in_specs=[vmem] * 2, out_specs=...  1.62 us

profile of v3, /device:TPU:1, one launch (start us, length us, event | category | flops | bytes accessed | tf_op | source)
XLA Modules:
  0.0 42.1 jit_solution(9947721479358648612)
XLA Ops:
  0.6 39.9 %shard_map.104 = (f32[32,768]{1,0:T(8,128)}, f32[32,768]{1,0:T(8,128)}) custom-call(bf16[77,32,768]{2,1,0:T(8,128)(2,1)} %bitcast.1, s32[2,4096]{1,0:T(2,128)} %layout.1, bf16[32,768]{1,0:T(8,128)(2,1)} %images.1, bf16[768,768]{1,0:T(8,128)(2,1)} %w_query.1, bf16[768,1536]{1,0:T(8,128)(2,1)} %w_keyval.1, bf16[768,768]{1,0:T(8,128)(2,1)} %w_out.1, ...), custom_call_target="tpu_custom_call" | custom-call | tf_op jit(solution)/shard_map/pallas_call | solution.py:499
  40.5 1.6 %shard_map.105 = (f32[32,768]{1,0:T(8,128)}, f32[32,768]{1,0:T(8,128)}) custom-call(f32[32,768]{1,0:T(8,128)} %get-tuple-element.4.image_from, f32[32,768]{1,0:T(8,128)} %get-tuple-element.5.text_from), custom_call_target="tpu_custom_call" | custom-call | tf_op jit(solution)/shard_map/pallas_call | solution.py:554

commit v4 on v3

--- a/solution.py
+++ b/solution.py
@@ -22,13 +22,14 @@
 BLOCK_HEADS = BLOCK // HEAD_DIM
 LOAD_STEPS = 7
 STEP_T = CTX // LOAD_STEPS
-NORM_UNROLL = 11
+LOOP_STEPS = 7
 CHIPS = 8
 ROWS = CHIPS * 2 * CAPS
 HALF = ROWS // 2
 PIECE = 128
 PIECES = ROWS // PIECE
 
+VMEM_LIMIT = 60 * 1024 * 1024
 LOGIT_SCALE = 100.0
 EPS_NORM = 1e-05
 EPS_UNIT = 1e-06
@@ -116,7 +117,8 @@
     tokens,
     normed,
     query_w,
-    keyval_w,
+    key_w,
+    value_w,
     out_w,
     up_w,
     down_w,
@@ -160,15 +162,12 @@
     load_counts = pltpu.make_async_copy(layout.at[:, span], counts, small_sem.at[0])
     load_images = pltpu.make_async_copy(images, image_rows, small_sem.at[1])
     load_ends = pltpu.make_async_copy(layout.at[:, span], ends, small_sem.at[2])
-    for step in range(LOAD_STEPS):
-        load(step).start()
-    for copy in (load_counts, load_ends, load_images):
-        copy.start()
     weights = {}
     for number, (name, source, target) in enumerate(
         (
             ("query", w_query, query_w),
-            ("keyval", w_keyval, keyval_w),
+            ("key", w_keyval.at[:, :WIDTH], key_w),
+            ("value", w_keyval.at[:, WIDTH:], value_w),
             ("out", w_out, out_w),
             ("up", w_up, up_w),
             ("down", w_down, down_w),
@@ -176,7 +175,12 @@
         )
     ):
         weights[name] = pltpu.make_async_copy(source, target, weight_sem.at[number])
-    weights["query"].start()
+    for step in range(LOAD_STEPS):
+        load(step).start()
+    for copy in (load_counts, load_ends, load_images):
+        copy.start()
+    for copy in weights.values():
+        copy.start(priority=1)
 
     barrier = pltpu.get_barrier_semaphore()
     friends = [partner]
@@ -188,82 +192,27 @@
 
     normed[:, TOKENS:, :] = jnp.zeros((GROUPS, TOKENS_PAD - TOKENS, WIDTH), BF16)
 
+
+    def norm_token(t):
+        at = t * GROUP if isinstance(t, int) else pl.multiple_of(t * GROUP, GROUP)
+        for group in range(GROUPS):
+            values = tokens[t, group * GROUP : (group + 1) * GROUP, :].astype(F32)
+            normed[group, pl.ds(at, GROUP), :] = norm_rows(values).astype(BF16)
+
     def norm_step(step, _):
         load(step).wait()
-
-        @pl.when(step == 1)
-        def _():
-            weights["keyval"].start()
-
-        @pl.when(step == 3)
-        def _():
-            for name in ("out", "up", "down", "proj"):
-                weights[name].start()
-
-        def token_step(inner, _):
-            t = step * STEP_T + inner
-            at = pl.ds(pl.multiple_of(t * GROUP, GROUP), GROUP)
-            for group in range(GROUPS):
-                rows = slice(group * GROUP, (group + 1) * GROUP)
-                values = tokens[t, rows, :].astype(F32)
-                normed[group, at, :] = norm_rows(values).astype(BF16)
-            return 0
-
-        return lax.fori_loop(0, STEP_T, token_step, 0, unroll=NORM_UNROLL)
-
-    lax.fori_loop(0, LOAD_STEPS, norm_step, 0)
-
-    load_images.wait()
-    image_values = image_rows[...].astype(F32)
-    image_unit = (image_values * unit_scale(image_values)).astype(BF16)
-    slots = (place.slot(0, 0), place.slot(1, 0))
-    units[0, 0, slots[0]] = image_unit
-
-    pl.semaphore_wait(barrier, len(friends))
-
-    def send_units(kind):
-        copies = {}
-        for offset in range(CHIPS - 1, 0, -1):
-            copies[offset] = pltpu.make_async_remote_copy(
-                src_ref=units.at[kind, 0, slots[kind]],
-                dst_ref=units.at[kind, 0, slots[kind]],
-                send_sem=gather_send.at[kind, offset],
-                recv_sem=gather_recv.at[kind, offset],
-                device_id=(place.peer(kind, offset, core),),
-                device_id_type=MESH,
-            )
-            copies[offset].start()
-        return copies
-
-    def hand_on(kind, offset):
-        slot = place.slot(kind, offset)
-        copy = pltpu.make_async_remote_copy(
-            src_ref=units.at[kind, 0, slot],
-            dst_ref=units.at[kind, 1, slot],
-            send_sem=pass_send.at[kind, offset],
-            recv_sem=pass_recv.at[kind, offset],
-            device_id=(partner,),
-            device_id_type=MESH,
-        )
-        copy.start()
-        return copy
-
-    image_sends = send_units(0)
-    passed = {(0, 0): hand_on(0, 0)}
-
+        for inner in range(STEP_T):
+            norm_token(step * STEP_T + inner)
+        return 0
+
+    lax.fori_loop(0, LOOP_STEPS, norm_step, 0)
+    for step in range(LOOP_STEPS, LOAD_STEPS):
+        load(step).wait()
+
+    load_ends.wait()
     load_counts.wait()
-    picked = iota((CAPS, 128), 1) == iota((CAPS, 128), 0) + me % 4 * CAPS
-    lengths = jnp.sum(jnp.where(picked, counts[0:1, :].astype(F32), 0.0), axis=1, keepdims=True)
-    lengths = jnp.maximum(lengths, 1.0)
-
-    token = iota((GROUP, TOKENS_PAD), 1)
-    own = token % GROUP == iota((GROUP, TOKENS_PAD), 0)
-    for group in range(GROUPS):
-        count = lengths[group * GROUP : (group + 1) * GROUP]
-        inside = own & ((token // GROUP).astype(F32) < count)
-        attn_bias[group] = jnp.where(inside, 0.0, -jnp.inf)
-
-    load_ends.wait()
+    weights["query"].wait()
+    weights["key"].wait()
     end_values = []
     for group in range(GROUPS):
         rows = jnp.zeros((GROUP, WIDTH), BF16)
@@ -275,21 +224,33 @@
         end_values.append(rows)
     end_values = jnp.concatenate(end_values, axis=0).astype(F32)
     end_normed = norm_rows(end_values).astype(BF16)
-    weights["query"].wait()
-    query = dot(end_normed, query_w[...]).astype(BF16).astype(F32) * (1.0 / math.sqrt(HEAD_DIM))
     head_of = iota((GROUP, BLOCK), 1) // HEAD_DIM
     groups = [slice(group * GROUP, (group + 1) * GROUP) for group in range(GROUPS)]
     spans = [slice(at, at + BLOCK) for at in range(0, WIDTH, BLOCK)]
-    weights["keyval"].wait()
     key_query = []
     for span in spans:
+        query = dot(end_normed, query_w[:, span]).astype(BF16).astype(F32)
+        query = query * (1.0 / math.sqrt(HEAD_DIM))
         spread = [
-            jnp.where(head_of == head, query[rows, span], 0.0)
+            jnp.where(head_of == head, query[rows], 0.0)
             for rows in groups
             for head in range(BLOCK_HEADS)
         ]
         spread = jnp.concatenate(spread, axis=0).astype(BF16)
-        key_query.append((dot_last(spread, keyval_w[:, span]) * LOG2_E).astype(BF16))
+        key_query.append((dot_last(spread, key_w[:, span]) * LOG2_E).astype(BF16))
+    for t in range(LOOP_STEPS * STEP_T, CTX):
+        norm_token(t)
+
+    picked = iota((CAPS, 128), 1) == iota((CAPS, 128), 0) + me % 4 * CAPS
+    lengths = jnp.sum(jnp.where(picked, counts[0:1, :].astype(F32), 0.0), axis=1, keepdims=True)
+    lengths = jnp.maximum(lengths, 1.0)
+
+    token = iota((GROUP, TOKENS_PAD), 1)
+    own = token % GROUP == iota((GROUP, TOKENS_PAD), 0)
+    for group in range(GROUPS):
+        count = lengths[group * GROUP : (group + 1) * GROUP]
+        inside = own & ((token // GROUP).astype(F32) < count)
+        attn_bias[group] = jnp.where(inside, 0.0, -jnp.inf)
 
     part = BLOCK_HEADS * GROUP
     contexts = []
@@ -307,11 +268,51 @@
         context = dot(attn[...], normed[group]) / jnp.concatenate(totals, axis=0)
         contexts.append(context.astype(BF16))
 
+    load_images.wait()
+    image_values = image_rows[...].astype(F32)
+    image_unit = (image_values * unit_scale(image_values)).astype(BF16)
+    slots = (place.slot(0, 0), place.slot(1, 0))
+    units[0, 0, slots[0]] = image_unit
+
+    pl.semaphore_wait(barrier, len(friends))
+
+    def send_units(kind):
+        copies = {}
+        for offset in range(CHIPS - 1, 0, -1):
+            copies[offset] = pltpu.make_async_remote_copy(
+                src_ref=units.at[kind, 0, slots[kind]],
+                dst_ref=units.at[kind, 0, slots[kind]],
+                send_sem=gather_send.at[kind, offset],
+                recv_sem=gather_recv.at[kind, offset],
+                device_id=(place.peer(kind, offset, core),),
+                device_id_type=MESH,
+            )
+            copies[offset].start()
+        return copies
+
+    def hand_on(kind, offset):
+        slot = place.slot(kind, offset)
+        copy = pltpu.make_async_remote_copy(
+            src_ref=units.at[kind, 0, slot],
+            dst_ref=units.at[kind, 1, slot],
+            send_sem=pass_send.at[kind, offset],
+            recv_sem=pass_recv.at[kind, offset],
+            device_id=(partner,),
+            device_id_type=MESH,
+        )
+        copy.start()
+        return copy
+
+    image_sends = send_units(0)
+    passed = {(0, 0): hand_on(0, 0)}
+
+    for name in ("value", "out", "up", "down", "proj"):
+        weights[name].wait()
     mixed = []
     for number, span in enumerate(spans):
         rows = slice(number * part, (number + 1) * part)
         by_head = jnp.concatenate([context[rows] for context in contexts], axis=0)
-        by_head = dot(by_head, keyval_w[:, WIDTH + span.start : WIDTH + span.stop])
+        by_head = dot(by_head, value_w[:, span])
         sums = []
         for group in range(GROUPS):
             total = jnp.zeros((GROUP, BLOCK), F32)
@@ -322,12 +323,9 @@
         mixed.append(jnp.concatenate(sums, axis=0))
     mixed = jnp.concatenate(mixed, axis=1).astype(BF16)
 
-    weights["out"].wait()
     residual = (end_values + dot(mixed, out_w[...])).astype(BF16)
     residual = residual.astype(F32)
     inner = norm_rows(residual).astype(BF16)
-    weights["up"].wait()
-    weights["down"].wait()
     final = residual
     for part in range(FF // WIDTH):
         span = slice(part * WIDTH, (part + 1) * WIDTH)
@@ -335,7 +333,6 @@
         hidden = 0.5 * hidden * (1.0 + lax.erf(hidden * (1.0 / math.sqrt(2.0))))
         final = final + dot(hidden.astype(BF16), down_w[span, :])
     pooled = norm_rows(final).astype(BF16)
-    weights["proj"].wait()
     text_values = dot(pooled, proj_w[...]).astype(BF16).astype(F32)
     text_unit = (text_values * unit_scale(text_values)).astype(BF16)
     units[1, 0, slots[1]] = text_unit
@@ -422,23 +419,27 @@
 
     part_sends = []
     for far in (1, 0):
-        for side in range(2):
-            first = place.slot(core, 4 * far) // 4 * 4
-            span = pl.ds(pl.multiple_of(side * HALF + first * CAPS, PIECE), PIECE)
-
-            def keep(grad):
-                blocks[side, pl.ds(first, 4)] = grad.astype(BF16).reshape(4, CAPS, WIDTH)
-
-            @pl.when(core == 0)
-            def _():
-                keep(dot_first(weight[:, span], units[1].reshape(ROWS, WIDTH)))
-
-            @pl.when(core == 1)
-            def _():
-                keep(dot(weight[span, :], units[0].reshape(ROWS, WIDTH)))
-
-            for offset in range(4 * far + 3, 4 * far - 1, -1):
-                slot = place.slot(core, offset)
+        first = place.slot(core, 4 * far) // 4 * 4
+        spans = [
+            pl.ds(pl.multiple_of(side * HALF + first * CAPS, PIECE), PIECE) for side in range(2)
+        ]
+
+        def keep(grad):
+            blocks[:, pl.ds(first, 4)] = grad.astype(BF16).reshape(2, 4, CAPS, WIDTH)
+
+        @pl.when(core == 0)
+        def _():
+            columns = jnp.concatenate([weight[:, span] for span in spans], axis=1)
+            keep(dot_first(columns, units[1].reshape(ROWS, WIDTH)))
+
+        @pl.when(core == 1)
+        def _():
+            rows = jnp.concatenate([weight[span, :] for span in spans], axis=0)
+            keep(dot(rows, units[0].reshape(ROWS, WIDTH)))
+
+        for offset in range(4 * far + 3, 4 * far - 1, -1):
+            slot = place.slot(core, offset)
+            for side in range(2):
                 if offset == 0 and side == 0:
                     parts[core, 0] = blocks[0, slot]
                     continue
@@ -498,14 +499,15 @@
     grads = (jax.ShapeDtypeStruct((CAPS, WIDTH), F32),) * 2
     made = pl.pallas_call(
         kernel,
-        out_shape=grads,
+        out_shape=(pltpu.VMEM((CAPS, WIDTH), F32),) * 2,
         in_specs=[hbm] * 9,
         out_specs=(vmem, vmem),
         scratch_shapes=[
             pltpu.VMEM((CTX, CAPS, WIDTH), BF16),
             pltpu.VMEM((GROUPS, TOKENS_PAD, WIDTH), BF16),
             pltpu.VMEM((WIDTH, WIDTH), BF16),
-            pltpu.VMEM((WIDTH, 2 * WIDTH), BF16),
+            pltpu.VMEM((WIDTH, WIDTH), BF16),
+            pltpu.VMEM((WIDTH, WIDTH), BF16),
             pltpu.VMEM((WIDTH, WIDTH), BF16),
             pltpu.VMEM((WIDTH, FF), BF16),
             pltpu.VMEM((FF, WIDTH), BF16),
@@ -527,7 +529,7 @@
             pltpu.VMEM((2, CHIPS, CAPS, WIDTH), BF16),
             dma((3,)),
             dma((LOAD_STEPS,)),
-            dma((6,)),
+            dma((7,)),
             dma((2, CHIPS)),
             dma((2, CHIPS)),
             dma((2, CHIPS)),
@@ -538,7 +540,7 @@
             dma((2, CHIPS)),
         ],
         compiler_params=pltpu.CompilerParams(
-            collective_id=0, has_side_effects=True, vmem_limit_bytes=60 * 1024 * 1024
+            collective_id=0, has_side_effects=True, vmem_limit_bytes=VMEM_LIMIT
         ),
     )(
         captions.transpose(1, 0, 2),
@@ -551,7 +553,13 @@
         w_down,
         w_proj,
     )
-    return pl.pallas_call(hand_out, out_shape=grads, in_specs=[vmem] * 2, out_specs=(vmem, vmem))(*made)
+    return pl.pallas_call(
+        hand_out,
+        out_shape=grads,
+        in_specs=[vmem] * 2,
+        out_specs=(vmem, vmem),
+        compiler_params=pltpu.CompilerParams(vmem_limit_bytes=4 * 1024 * 1024),
+    )(*made)
 
 
 def solution(mesh):

time: 42.3 us -> 39.6 us (0.936)
  Pallas kernels: 41.5 us -> 38.8 us
    pallas_call x1, Pallas kernels: 39.9 us -> 38.1 us  [body(): pl.pallas_call(kernel, out_shape=(pltpu.VMEM((CAPS, WIDTH), F32),) * 2, i...]
    pallas_call x1, Pallas kernels: 1.62 us -> 0.69 us  [body(): pl.pallas_call(hand_out, out_shape=grads, in_specs=[vmem] * 2, out_specs=...]
where the time goes in v4:
time: 39.6 us; the launch traced here: 39.5 us
  Pallas kernels  38.8 us (98%)
  between operations  0.64 us (2%)
    pallas_call x1, Pallas kernels, body(): pl.pallas_call(kernel, out_shape=(pltpu.VMEM((CAPS, WIDTH), F32),) * 2, i...  38.1 us

profile of v4, /device:TPU:1, one launch (start us, length us, event | category | flops | bytes accessed | tf_op | source)
XLA Modules:
  0.0 39.5 jit_solution(15990420183663127475)
XLA Ops:
  0.6 38.1 %shard_map.104 = (f32[32,768]{1,0:T(8,128)S(1)}, f32[32,768]{1,0:T(8,128)S(1)}) custom-call(bf16[77,32,768]{2,1,0:T(8,128)(2,1)} %bitcast.1, s32[2,4096]{1,0:T(2,128)} %layout.1, bf16[32,768]{1,0:T(8,128)(2,1)} %images.1, bf16[768,768]{1,0:T(8,128)(2,1)} %w_query.1, bf16[768,1536]{1,0:T(8,128)(2,1)} %w_keyval.1, bf16[768,768]{1,0:T(8,128)(2,1)} %w_out.1, ...), custom_call_target="tpu_custom_call" | custom-call | tf_op jit(solution)/shard_map/pallas_call | solution.py:500
  38.8 0.7 %shard_map.105 = (f32[32,768]{1,0:T(8,128)}, f32[32,768]{1,0:T(8,128)}) custom-call(f32[32,768]{1,0:T(8,128)S(1)} %get-tuple-element.4.image_from, f32[32,768]{1,0:T(8,128)S(1)} %get-tuple-element.5.text_from), custom_call_target="tpu_custom_call" | custom-call | tf_op jit(solution)/shard_map/pallas_call | solution.py:556

commit v5 on v4

--- a/solution.py
+++ b/solution.py
@@ -24,6 +24,7 @@
 STEP_T = CTX // LOAD_STEPS
 LOOP_STEPS = 7
 CHIPS = 8
+ARRIVAL = (7, 1, 6, 3, 2, 5, 4)
 ROWS = CHIPS * 2 * CAPS
 HALF = ROWS // 2
 PIECE = 128
@@ -152,7 +153,6 @@
 ):
     place = Place()
     me, core, partner = place.me, place.core, place.partner
-    other = 1 - core
 
     def load(step):
         span = pl.ds(step * STEP_T, STEP_T)
@@ -257,15 +257,16 @@
     for group in range(GROUPS):
         rows = slice(group * part, (group + 1) * part)
         asked = jnp.concatenate([block[rows] for block in key_query], axis=0)
-        attn_scores[...] = dot_last(asked, normed[group])
+        attn_scores[group] = dot_last(asked, normed[group])
+    for group in range(GROUPS):
         totals = []
         for head in range(HEADS):
             rows = slice(head * GROUP, (head + 1) * GROUP)
-            value = attn_scores[rows, :] + attn_bias[group]
+            value = attn_scores[group, rows, :] + attn_bias[group]
             value = jnp.exp2(value - jnp.max(value, axis=1, keepdims=True))
-            attn[rows, :] = value.astype(BF16)
+            attn[group, rows, :] = value.astype(BF16)
             totals.append(jnp.sum(value, axis=1, keepdims=True))
-        context = dot(attn[...], normed[group]) / jnp.concatenate(totals, axis=0)
+        context = dot(attn[group], normed[group]) / jnp.concatenate(totals, axis=0)
         contexts.append(context.astype(BF16))
 
     load_images.wait()
@@ -344,7 +345,7 @@
         image_sends[offset].wait_recv()
         passed[0, offset] = hand_on(0, offset)
 
-    for offset in range(CHIPS - 1, 0, -1):
+    for offset in ARRIVAL:
         text_sends[offset].wait_recv()
         passed[1, offset] = hand_on(1, offset)
     for offset in range(CHIPS):
@@ -417,9 +418,10 @@
             both = row_exp[half, rows] * row_scale + col_exp[half, rows] * col_scale
             weight[first : first + PIECE, :] = both.astype(BF16)
 
+    duty = 1 - core
     part_sends = []
     for far in (1, 0):
-        first = place.slot(core, 4 * far) // 4 * 4
+        first = place.slot(duty, 4 * far) // 4 * 4
         spans = [
             pl.ds(pl.multiple_of(side * HALF + first * CAPS, PIECE), PIECE) for side in range(2)
         ]
@@ -427,28 +429,28 @@
         def keep(grad):
             blocks[:, pl.ds(first, 4)] = grad.astype(BF16).reshape(2, 4, CAPS, WIDTH)
 
-        @pl.when(core == 0)
+        @pl.when(duty == 0)
         def _():
             columns = jnp.concatenate([weight[:, span] for span in spans], axis=1)
             keep(dot_first(columns, units[1].reshape(ROWS, WIDTH)))
 
-        @pl.when(core == 1)
+        @pl.when(duty == 1)
         def _():
             rows = jnp.concatenate([weight[span, :] for span in spans], axis=0)
             keep(dot(rows, units[0].reshape(ROWS, WIDTH)))
 
         for offset in range(4 * far + 3, 4 * far - 1, -1):
-            slot = place.slot(core, offset)
+            slot = place.slot(duty, offset)
             for side in range(2):
                 if offset == 0 and side == 0:
-                    parts[core, 0] = blocks[0, slot]
+                    parts[duty, 0] = blocks[0, slot]
                     continue
                 copy = pltpu.make_async_remote_copy(
                     src_ref=blocks.at[side, slot],
-                    dst_ref=parts.at[core, offset],
+                    dst_ref=parts.at[duty, offset],
                     send_sem=part_send.at[offset, side],
-                    recv_sem=part_recv.at[core, offset],
-                    device_id=(place.peer(core, offset, core + side - 2 * side * core),),
+                    recv_sem=part_recv.at[duty, offset],
+                    device_id=(place.peer(duty, offset, core + side - 2 * side * core),),
                     device_id_type=MESH,
                 )
                 copy.start()
@@ -464,7 +466,7 @@
             device_id_type=MESH,
         ).wait_recv()
 
-    arrived(other, 0)
+    arrived(core, 0)
     for offset in range(1, CHIPS):
         for kind in range(2):
             arrived(kind, offset)
@@ -515,9 +517,9 @@
             pltpu.VMEM((2, 128), jnp.int32),
             pltpu.SMEM((2, 128), jnp.int32),
             pltpu.VMEM((CAPS, WIDTH), BF16),
-            pltpu.VMEM((SPLIT, TOKENS_PAD), F32),
+            pltpu.VMEM((GROUPS, SPLIT, TOKENS_PAD), F32),
             pltpu.VMEM((GROUPS, GROUP, TOKENS_PAD), F32),
-            pltpu.VMEM((SPLIT, TOKENS_PAD), BF16),
+            pltpu.VMEM((GROUPS, SPLIT, TOKENS_PAD), BF16),
             pltpu.VMEM((2, 2, CHIPS, CAPS, WIDTH), BF16),
             pltpu.VMEM((2, HALF, ROWS), F32),
             pltpu.VMEM((2, HALF, ROWS), F32),

time: 39.6 us -> 38.7 us (0.977)
  Pallas kernels: 38.8 us -> 37.9 us
    pallas_call x1, Pallas kernels: 38.1 us -> 37.2 us  [body(): pl.pallas_call(kernel, out_shape=(pltpu.VMEM((CAPS, WIDTH), F32),) * 2, i...]
where the time goes in v5:
time: 38.7 us; the launch traced here: 38.6 us
  Pallas kernels  37.9 us (98%)
  between operations  0.64 us (2%)
    pallas_call x1, Pallas kernels, body(): pl.pallas_call(kernel, out_shape=(pltpu.VMEM((CAPS, WIDTH), F32),) * 2, i...  37.2 us

profile of v5, /device:TPU:1, one launch (start us, length us, event | category | flops | bytes accessed | tf_op | source)
XLA Modules:
  0.0 38.6 jit_solution(183077253054037793)
XLA Ops:
  0.6 37.2 %shard_map.104 = (f32[32,768]{1,0:T(8,128)S(1)}, f32[32,768]{1,0:T(8,128)S(1)}) custom-call(bf16[77,32,768]{2,1,0:T(8,128)(2,1)} %bitcast.1, s32[2,4096]{1,0:T(2,128)} %layout.1, bf16[32,768]{1,0:T(8,128)(2,1)} %images.1, bf16[768,768]{1,0:T(8,128)(2,1)} %w_query.1, bf16[768,1536]{1,0:T(8,128)(2,1)} %w_keyval.1, bf16[768,768]{1,0:T(8,128)(2,1)} %w_out.1, ...), custom_call_target="tpu_custom_call" | custom-call | tf_op jit(solution)/shard_map/pallas_call | solution.py:502
  37.9 0.7 %shard_map.105 = (f32[32,768]{1,0:T(8,128)}, f32[32,768]{1,0:T(8,128)}) custom-call(f32[32,768]{1,0:T(8,128)S(1)} %get-tuple-element.4.image_from, f32[32,768]{1,0:T(8,128)S(1)} %get-tuple-element.5.text_from), custom_call_target="tpu_custom_call" | custom-call | tf_op jit(solution)/shard_map/pallas_call | solution.py:558

commit v6 on v5

--- a/solution.py
+++ b/solution.py
@@ -13,16 +13,19 @@
 CTX = 77
 CAPS = 32
 FF = 3072
-GROUP = 16
+TILE = 16
+GROUP = 8
 GROUPS = CAPS // GROUP
 SPLIT = HEADS * GROUP
-TOKENS = CTX * GROUP
-TOKENS_PAD = -(-TOKENS // 256) * 256
+PAIRS = (CTX + 1) // 2
+TOKENS = PAIRS * 2 * GROUP
+TOKENS_PAD = -(-TOKENS // 128) * 128
 BLOCK = 256
 BLOCK_HEADS = BLOCK // HEAD_DIM
-LOAD_STEPS = 7
-STEP_T = CTX // LOAD_STEPS
-LOOP_STEPS = 7
+BLOCKS = WIDTH // BLOCK
+LOAD_STEPS = 6
+STEP_T = 12
+TAIL = CTX - LOAD_STEPS * STEP_T
 CHIPS = 8
 ARRIVAL = (7, 1, 6, 3, 2, 5, 4)
 ROWS = CHIPS * 2 * CAPS
@@ -154,8 +157,8 @@
     place = Place()
     me, core, partner = place.me, place.core, place.partner
 
-    def load(step):
-        span = pl.ds(step * STEP_T, STEP_T)
+    def load(step, size=STEP_T):
+        span = pl.ds(step * STEP_T, size)
         return pltpu.make_async_copy(captions.at[span], tokens.at[span], load_sem.at[step])
 
     span = pl.ds(pl.multiple_of(me // 4 * 128, 128), 128)
@@ -177,6 +180,8 @@
         weights[name] = pltpu.make_async_copy(source, target, weight_sem.at[number])
     for step in range(LOAD_STEPS):
         load(step).start()
+    load_tail = load(LOAD_STEPS, TAIL)
+    load_tail.start()
     for copy in (load_counts, load_ends, load_images):
         copy.start()
     for copy in weights.values():
@@ -191,36 +196,42 @@
         pl.semaphore_signal(barrier, inc=1, device_id=(friend,), device_id_type=MESH)
 
     normed[:, TOKENS:, :] = jnp.zeros((GROUPS, TOKENS_PAD - TOKENS, WIDTH), BF16)
-
-
-    def norm_token(t):
-        at = t * GROUP if isinstance(t, int) else pl.multiple_of(t * GROUP, GROUP)
-        for group in range(GROUPS):
-            values = tokens[t, group * GROUP : (group + 1) * GROUP, :].astype(F32)
-            normed[group, pl.ds(at, GROUP), :] = norm_rows(values).astype(BF16)
+    tokens[CTX] = jnp.zeros((CAPS, WIDTH), BF16)
+
+
+    def norm_pair(pair):
+        at = pair * TILE if isinstance(pair, int) else pl.multiple_of(pair * TILE, TILE)
+        for tile in range(0, CAPS, TILE):
+            halves = [
+                norm_rows(tokens[2 * pair + side, tile : tile + TILE, :].astype(F32))
+                for side in range(2)
+            ]
+            for first in range(0, TILE, GROUP):
+                rows = jnp.concatenate([half[first : first + GROUP] for half in halves], axis=0)
+                normed[(tile + first) // GROUP, pl.ds(at, TILE), :] = rows.astype(BF16)
 
     def norm_step(step, _):
         load(step).wait()
-        for inner in range(STEP_T):
-            norm_token(step * STEP_T + inner)
+        for inner in range(STEP_T // 2):
+            norm_pair(step * (STEP_T // 2) + inner)
         return 0
 
-    lax.fori_loop(0, LOOP_STEPS, norm_step, 0)
-    for step in range(LOOP_STEPS, LOAD_STEPS):
-        load(step).wait()
+    lax.fori_loop(0, LOAD_STEPS, norm_step, 0)
+    load_tail.wait()
+    for pair in range(LOAD_STEPS * STEP_T // 2, PAIRS):
+        norm_pair(pair)
 
     load_ends.wait()
     load_counts.wait()
     weights["query"].wait()
     weights["key"].wait()
     end_values = []
-    for group in range(GROUPS):
-        rows = jnp.zeros((GROUP, WIDTH), BF16)
-        for inner in range(GROUP):
-            caption = group * GROUP + inner
-            last = jnp.clip(ends[0, me % 4 * CAPS + caption] - 1, 0, CTX - 1)
-            found = tokens[last, group * GROUP : (group + 1) * GROUP, :]
-            rows = jnp.where(iota((GROUP, WIDTH), 0) == inner, found, rows)
+    for first in range(0, CAPS, TILE):
+        rows = jnp.zeros((TILE, WIDTH), BF16)
+        for inner in range(TILE):
+            last = jnp.clip(ends[0, me % 4 * CAPS + first + inner] - 1, 0, CTX - 1)
+            found = tokens[last, first : first + TILE, :]
+            rows = jnp.where(iota((TILE, WIDTH), 0) == inner, found, rows)
         end_values.append(rows)
     end_values = jnp.concatenate(end_values, axis=0).astype(F32)
     end_normed = norm_rows(end_values).astype(BF16)
@@ -238,17 +249,16 @@
         ]
         spread = jnp.concatenate(spread, axis=0).astype(BF16)
         key_query.append((dot_last(spread, key_w[:, span]) * LOG2_E).astype(BF16))
-    for t in range(LOOP_STEPS * STEP_T, CTX):
-        norm_token(t)
 
     picked = iota((CAPS, 128), 1) == iota((CAPS, 128), 0) + me % 4 * CAPS
     lengths = jnp.sum(jnp.where(picked, counts[0:1, :].astype(F32), 0.0), axis=1, keepdims=True)
     lengths = jnp.maximum(lengths, 1.0)
 
-    token = iota((GROUP, TOKENS_PAD), 1)
-    own = token % GROUP == iota((GROUP, TOKENS_PAD), 0)
+    token = iota((2 * GROUP, TOKENS_PAD), 1)
+    own = token % GROUP == iota((2 * GROUP, TOKENS_PAD), 0) % GROUP
     for group in range(GROUPS):
         count = lengths[group * GROUP : (group + 1) * GROUP]
+        count = jnp.concatenate([count, count], axis=0)
         inside = own & ((token // GROUP).astype(F32) < count)
         attn_bias[group] = jnp.where(inside, 0.0, -jnp.inf)
 
@@ -260,8 +270,8 @@
         attn_scores[group] = dot_last(asked, normed[group])
     for group in range(GROUPS):
         totals = []
-        for head in range(HEADS):
-            rows = slice(head * GROUP, (head + 1) * GROUP)
+        for head in range(0, HEADS, 2):
+            rows = slice(head * GROUP, (head + 2) * GROUP)
             value = attn_scores[group, rows, :] + attn_bias[group]
             value = jnp.exp2(value - jnp.max(value, axis=1, keepdims=True))
             attn[group, rows, :] = value.astype(BF16)
@@ -505,7 +515,7 @@
         in_specs=[hbm] * 9,
         out_specs=(vmem, vmem),
         scratch_shapes=[
-            pltpu.VMEM((CTX, CAPS, WIDTH), BF16),
+            pltpu.VMEM((CTX + 1, CAPS, WIDTH), BF16),
             pltpu.VMEM((GROUPS, TOKENS_PAD, WIDTH), BF16),
             pltpu.VMEM((WIDTH, WIDTH), BF16),
             pltpu.VMEM((WIDTH, WIDTH), BF16),
@@ -518,7 +528,7 @@
             pltpu.SMEM((2, 128), jnp.int32),
             pltpu.VMEM((CAPS, WIDTH), BF16),
             pltpu.VMEM((GROUPS, SPLIT, TOKENS_PAD), F32),
-            pltpu.VMEM((GROUPS, GROUP, TOKENS_PAD), F32),
+            pltpu.VMEM((GROUPS, 2 * GROUP, TOKENS_PAD), F32),
             pltpu.VMEM((GROUPS, SPLIT, TOKENS_PAD), BF16),
             pltpu.VMEM((2, 2, CHIPS, CAPS, WIDTH), BF16),
             pltpu.VMEM((2, HALF, ROWS), F32),
@@ -530,7 +540,7 @@
             pltpu.VMEM((2, CHIPS, CAPS, WIDTH), BF16),
             pltpu.VMEM((2, CHIPS, CAPS, WIDTH), BF16),
             dma((3,)),
-            dma((LOAD_STEPS,)),
+            dma((LOAD_STEPS + 1,)),
             dma((7,)),
             dma((2, CHIPS)),
             dma((2, CHIPS)),

time: 38.7 us -> 38.4 us (level)
  no operation moved by 1% of the time
where the time goes in v6:
time: 38.4 us; the launch traced here: 38.3 us
  Pallas kernels  37.7 us (98%)
  between operations  0.64 us (2%)
    pallas_call x1, Pallas kernels, body(): pl.pallas_call(kernel, out_shape=(pltpu.VMEM((CAPS, WIDTH), F32),) * 2, i...  37 us

profile of v6, /device:TPU:1, one launch (start us, length us, event | category | flops | bytes accessed | tf_op | source)
XLA Modules:
  0.0 38.3 jit_solution(487003789016744110)
XLA Ops:
  0.6 37.0 %shard_map.104 = (f32[32,768]{1,0:T(8,128)S(1)}, f32[32,768]{1,0:T(8,128)S(1)}) custom-call(bf16[77,32,768]{2,1,0:T(8,128)(2,1)} %bitcast.1, s32[2,4096]{1,0:T(2,128)} %layout.1, bf16[32,768]{1,0:T(8,128)(2,1)} %images.1, bf16[768,768]{1,0:T(8,128)(2,1)} %w_query.1, bf16[768,1536]{1,0:T(8,128)(2,1)} %w_keyval.1, bf16[768,768]{1,0:T(8,128)(2,1)} %w_out.1, ...), custom_call_target="tpu_custom_call" | custom-call | tf_op jit(solution)/shard_map/pallas_call | solution.py:512
  37.6 0.7 %shard_map.105 = (f32[32,768]{1,0:T(8,128)}, f32[32,768]{1,0:T(8,128)}) custom-call(f32[32,768]{1,0:T(8,128)S(1)} %get-tuple-element.4.image_from, f32[32,768]{1,0:T(8,128)S(1)} %get-tuple-element.5.text_from), custom_call_target="tpu_custom_call" | custom-call | tf_op jit(solution)/shard_map/pallas_call | solution.py:568

commit v7 on v6

--- a/solution.py
+++ b/solution.py
@@ -138,7 +138,8 @@
     col_exp,
     row_peak,
     col_peak,
-    logs,
+    image_logs,
+    text_logs,
     weight,
     blocks,
     parts,
@@ -362,68 +363,72 @@
         passed[0, offset].wait_recv()
 
     eye = iota((PIECE, PIECE), 0) == iota((PIECE, PIECE), 1)
-    col_sums, col_peaks = [], []
-    for half in range(2):
-        if half == 1:
-            for offset in range(CHIPS):
-                passed[1, offset].wait_recv()
+    half_pieces = HALF // PIECE
+
+    def score(half):
         scores = dot_last(units[1, half].reshape(HALF, WIDTH), units[0].reshape(ROWS, WIDTH))
         scores = scores * (LOGIT_SCALE * LOG2_E)
-        peak = jnp.max(scores, axis=1, keepdims=True)
-        value = jnp.exp2(scores - peak)
-        row_exp[half] = value
-        row_peak[half] = peak
-        log = peak + jnp.log(jnp.sum(value, axis=1, keepdims=True)) * LOG2_E
-        for piece in range(HALF // PIECE):
-            part = log[piece * PIECE : (piece + 1) * PIECE]
-            part = jnp.sum(jnp.where(eye, part, 0.0), axis=0, keepdims=True)
-            logs[1, 0, half * (HALF // PIECE) + piece] = part
-        peak = jnp.max(scores, axis=0, keepdims=True)
-        value = jnp.exp2(scores - peak)
-        col_exp[half] = value
-        col_peak[half] = peak
-        col_peaks.append(peak)
-        col_sums.append(jnp.sum(value, axis=0, keepdims=True))
-    top = jnp.maximum(*col_peaks)
-    total = sum(part * jnp.exp2(peak - top) for part, peak in zip(col_sums, col_peaks))
-    log = top + jnp.log(total) * LOG2_E
+        for axis, exp, top in ((1, row_exp, row_peak), (0, col_exp, col_peak)):
+            peak = jnp.max(scores, axis=axis, keepdims=True)
+            value = jnp.exp2(scores - peak)
+            exp[half] = value
+            top[half] = peak
+            if half == 0:
+                yield peak + jnp.log(jnp.sum(value, axis=axis, keepdims=True)) * LOG2_E
+
+    row_log, col_log = score(0)
+    for piece in range(half_pieces):
+        part = row_log[piece * PIECE : (piece + 1) * PIECE]
+        part = jnp.sum(jnp.where(eye, part, 0.0), axis=0, keepdims=True)
+        text_logs[0, 0, piece] = part
     for piece in range(PIECES):
-        logs[0, 0, piece] = log[:, piece * PIECE : (piece + 1) * PIECE]
+        image_logs[0, 0, piece] = col_log[:, piece * PIECE : (piece + 1) * PIECE]
 
     log_sends = []
-    for offset in range(CHIPS - 1, 0, -1):
-        for kind in range(2):
-            copy = pltpu.make_async_remote_copy(
-                src_ref=logs.at[kind, 0],
-                dst_ref=logs.at[kind, offset],
-                send_sem=log_send.at[kind, offset],
-                recv_sem=log_recv.at[kind, offset],
-                device_id=(place.peer(kind, offset, core),),
-                device_id_type=MESH,
-            )
-            copy.start()
-            log_sends.append(copy)
+    for offset in range(CHIPS - 1, -1, -1):
+        for kind, logs in enumerate((image_logs, text_logs)):
+            for side in range(2):
+                if offset == 0 and side == 0:
+                    continue
+                copy = pltpu.make_async_remote_copy(
+                    src_ref=logs.at[0, 0],
+                    dst_ref=logs.at[side, offset],
+                    send_sem=log_send.at[kind, side, offset],
+                    recv_sem=log_recv.at[kind, side, offset],
+                    device_id=(place.peer(kind, offset, core + side - 2 * side * core),),
+                    device_id_type=MESH,
+                )
+                copy.start()
+                log_sends.append(copy)
+
+    for offset in range(CHIPS):
+        passed[1, offset].wait_recv()
+    for _ in score(1):
+        pass
+
     for copy in log_sends:
         copy.wait_recv()
 
-    def whole_log(kind):
-        top = logs[kind, 0]
-        for offset in range(1, CHIPS):
-            top = jnp.maximum(top, logs[kind, offset])
-        total = jnp.zeros_like(top)
-        for offset in range(CHIPS):
-            total = total + jnp.exp2(logs[kind, offset] - top)
+    def whole_log(terms):
+        top = terms[0]
+        for term in terms[1:]:
+            top = jnp.maximum(top, term)
+        total = sum(jnp.exp2(term - top) for term in terms)
         return top + jnp.log(total) * LOG2_E
 
-    image_logs, text_logs = whole_log(0), whole_log(1)
-    image_logs = jnp.concatenate([image_logs[piece] for piece in range(PIECES)], axis=1)
+    terms = [image_logs[0, offset] for offset in range(CHIPS)]
+    for offset in range(CHIPS):
+        term = image_logs[1, offset]
+        terms.append(jnp.concatenate([term[half_pieces:], term[:half_pieces]], axis=0))
+    image_log = whole_log(terms)
+    image_log = jnp.concatenate([image_log[piece] for piece in range(PIECES)], axis=1)
     for half in range(2):
-        col_scale = jnp.exp2(col_peak[half] - image_logs)
-        for piece in range(HALF // PIECE):
+        text_log = whole_log([text_logs[half, offset] for offset in range(CHIPS)])
+        col_scale = jnp.exp2(col_peak[half] - image_log)
+        for piece in range(half_pieces):
             rows = slice(piece * PIECE, (piece + 1) * PIECE)
             first = half * HALF + piece * PIECE
-            log = text_logs[half * (HALF // PIECE) + piece]
-            log = jnp.sum(jnp.where(eye, log, 0.0), axis=1, keepdims=True)
+            log = jnp.sum(jnp.where(eye, text_log[piece], 0.0), axis=1, keepdims=True)
             row_scale = jnp.exp2(row_peak[half, rows] - log)
             both = row_exp[half, rows] * row_scale + col_exp[half, rows] * col_scale
             weight[first : first + PIECE, :] = both.astype(BF16)
@@ -536,6 +541,7 @@
             pltpu.VMEM((2, HALF, 1), F32),
             pltpu.VMEM((2, 1, ROWS), F32),
             pltpu.VMEM((2, CHIPS, PIECES, 1, PIECE), F32),
+            pltpu.VMEM((2, CHIPS, HALF // PIECE, 1, PIECE), F32),
             pltpu.VMEM((ROWS, ROWS), BF16),
             pltpu.VMEM((2, CHIPS, CAPS, WIDTH), BF16),
             pltpu.VMEM((2, CHIPS, CAPS, WIDTH), BF16),
@@ -546,8 +552,8 @@
             dma((2, CHIPS)),
             dma((2, CHIPS)),
             dma((2, CHIPS)),
-            dma((2, CHIPS)),
-            dma((2, CHIPS)),
+            dma((2, 2, CHIPS)),
+            dma((2, 2, CHIPS)),
             dma((CHIPS, 2)),
             dma((2, CHIPS)),
         ],

time: 38.4 us -> 38.1 us (level)
  no operation moved by 1% of the time
where the time goes in v7:
time: 38.1 us; the launch traced here: 38 us
  Pallas kernels  37.4 us (98%)
  between operations  0.64 us (2%)
    pallas_call x1, Pallas kernels, body(): pl.pallas_call(kernel, out_shape=(pltpu.VMEM((CAPS, WIDTH), F32),) * 2, i...  36.7 us

profile of v7, /device:TPU:1, one launch (start us, length us, event | category | flops | bytes accessed | tf_op | source)
XLA Modules:
  0.0 38.0 jit_solution(7528093718277611054)
XLA Ops:
  0.6 36.7 %shard_map.104 = (f32[32,768]{1,0:T(8,128)S(1)}, f32[32,768]{1,0:T(8,128)S(1)}) custom-call(bf16[77,32,768]{2,1,0:T(8,128)(2,1)} %bitcast.1, s32[2,4096]{1,0:T(2,128)} %layout.1, bf16[32,768]{1,0:T(8,128)(2,1)} %images.1, bf16[768,768]{1,0:T(8,128)(2,1)} %w_query.1, bf16[768,1536]{1,0:T(8,128)(2,1)} %w_keyval.1, bf16[768,768]{1,0:T(8,128)(2,1)} %w_out.1, ...), custom_call_target="tpu_custom_call" | custom-call | tf_op jit(solution)/shard_map/pallas_call | solution.py:517
  37.3 0.7 %shard_map.105 = (f32[32,768]{1,0:T(8,128)}, f32[32,768]{1,0:T(8,128)}) custom-call(f32[32,768]{1,0:T(8,128)S(1)} %get-tuple-element.4.image_from, f32[32,768]{1,0:T(8,128)S(1)} %get-tuple-element.5.text_from), custom_call_target="tpu_custom_call" | custom-call | tf_op jit(solution)/shard_map/pallas_call | solution.py:574

commit v8 on v7

--- a/solution.py
+++ b/solution.py
@@ -34,6 +34,7 @@
 PIECES = ROWS // PIECE
 
 VMEM_LIMIT = 60 * 1024 * 1024
+TEXT_OUTER = "y"
 LOGIT_SCALE = 100.0
 EPS_NORM = 1e-05
 EPS_UNIT = 1e-06
@@ -83,16 +84,19 @@
         self.at = {"y": (self.me // 2) % 4, "z": (self.me // 8) % 4, "x": self.me // 32}
         self.partner = self.me + 1 - 2 * self.core
 
-    def flip(self, kind, value):
-        image, text = 3 - value, value + 1 - 2 * (value % 2)
-        return image + kind * (text - image)
-
-    def bit(self, kind, value):
+    def flip(self, kind, axis):
+        value = self.at[axis]
+        outer, inner = 3 - value, value + 1 - 2 * (value % 2)
+        kind = 1 - kind if axis in TEXT_OUTER else kind
+        return outer + kind * (inner - outer)
+
+    def bit(self, kind, axis, value):
+        kind = 1 - kind if axis in TEXT_OUTER else kind
         return value // 2 + kind * (value % 2 - value // 2)
 
     def coords(self, kind, offset):
         return {
-            axis: self.flip(kind, self.at[axis]) if offset >> step & 1 else self.at[axis]
+            axis: self.flip(kind, axis) if offset >> step & 1 else self.at[axis]
             for step, axis in enumerate("yzx")
         }
 
@@ -102,7 +106,7 @@
 
     def slot(self, kind, offset):
         where = self.coords(kind, offset)
-        bits = {axis: self.bit(kind, where[axis]) for axis in "yzx"}
+        bits = {axis: self.bit(kind, axis, where[axis]) for axis in "yzx"}
         return bits["x"] * 4 + bits["z"] * 2 + bits["y"]
 
 
@@ -152,8 +156,7 @@
     pass_recv,
     log_send,
     log_recv,
-    part_send,
-    part_recv,
+    part_sem,
 ):
     place = Place()
     me, core, partner = place.me, place.core, place.partner
@@ -286,6 +289,16 @@
     slots = (place.slot(0, 0), place.slot(1, 0))
     units[0, 0, slots[0]] = image_unit
 
+    def all_of(buffer, semaphore):
+        return pltpu.make_async_remote_copy(
+            src_ref=buffer,
+            dst_ref=buffer,
+            send_sem=semaphore,
+            recv_sem=semaphore,
+            device_id=(partner,),
+            device_id_type=MESH,
+        )
+
     pl.semaphore_wait(barrier, len(friends))
 
     def send_units(kind):
@@ -294,8 +307,8 @@
             copies[offset] = pltpu.make_async_remote_copy(
                 src_ref=units.at[kind, 0, slots[kind]],
                 dst_ref=units.at[kind, 0, slots[kind]],
-                send_sem=gather_send.at[kind, offset],
-                recv_sem=gather_recv.at[kind, offset],
+                send_sem=gather_send.at[kind],
+                recv_sem=gather_recv.at[offset] if kind else gather_recv.at[0],
                 device_id=(place.peer(kind, offset, core),),
                 device_id_type=MESH,
             )
@@ -307,16 +320,15 @@
         copy = pltpu.make_async_remote_copy(
             src_ref=units.at[kind, 0, slot],
             dst_ref=units.at[kind, 1, slot],
-            send_sem=pass_send.at[kind, offset],
-            recv_sem=pass_recv.at[kind, offset],
+            send_sem=pass_send.at[kind],
+            recv_sem=pass_recv.at[kind],
             device_id=(partner,),
             device_id_type=MESH,
         )
         copy.start()
-        return copy
-
-    image_sends = send_units(0)
-    passed = {(0, 0): hand_on(0, 0)}
+
+    send_units(0)
+    hand_on(0, 0)
 
     for name in ("value", "out", "up", "down", "proj"):
         weights[name].wait()
@@ -350,17 +362,16 @@
     units[1, 0, slots[1]] = text_unit
 
     text_sends = send_units(1)
-    passed[1, 0] = hand_on(1, 0)
-
+    hand_on(1, 0)
+
+    all_of(units.at[0, 0, pl.ds(0, CHIPS - 1)], gather_recv.at[0]).wait_recv()
     for offset in range(1, CHIPS):
-        image_sends[offset].wait_recv()
-        passed[0, offset] = hand_on(0, offset)
+        hand_on(0, offset)
 
     for offset in ARRIVAL:
         text_sends[offset].wait_recv()
-        passed[1, offset] = hand_on(1, offset)
-    for offset in range(CHIPS):
-        passed[0, offset].wait_recv()
+        hand_on(1, offset)
+    all_of(units.at[0, 1], pass_recv.at[0]).wait_recv()
 
     eye = iota((PIECE, PIECE), 0) == iota((PIECE, PIECE), 1)
     half_pieces = HALF // PIECE
@@ -380,34 +391,32 @@
     for piece in range(half_pieces):
         part = row_log[piece * PIECE : (piece + 1) * PIECE]
         part = jnp.sum(jnp.where(eye, part, 0.0), axis=0, keepdims=True)
-        text_logs[0, 0, piece] = part
+        text_logs[0, piece] = part
     for piece in range(PIECES):
-        image_logs[0, 0, piece] = col_log[:, piece * PIECE : (piece + 1) * PIECE]
-
-    log_sends = []
+        image_logs[0, piece] = col_log[:, piece * PIECE : (piece + 1) * PIECE]
+
     for offset in range(CHIPS - 1, -1, -1):
         for kind, logs in enumerate((image_logs, text_logs)):
             for side in range(2):
                 if offset == 0 and side == 0:
                     continue
                 copy = pltpu.make_async_remote_copy(
-                    src_ref=logs.at[0, 0],
-                    dst_ref=logs.at[side, offset],
-                    send_sem=log_send.at[kind, side, offset],
-                    recv_sem=log_recv.at[kind, side, offset],
+                    src_ref=logs.at[0],
+                    dst_ref=logs.at[side * CHIPS + offset],
+                    send_sem=log_send.at[kind],
+                    recv_sem=log_recv.at[kind],
                     device_id=(place.peer(kind, offset, core + side - 2 * side * core),),
                     device_id_type=MESH,
                 )
                 copy.start()
-                log_sends.append(copy)
-
-    for offset in range(CHIPS):
-        passed[1, offset].wait_recv()
+
+    all_of(units.at[1, 1], pass_recv.at[1]).wait_recv()
     for _ in score(1):
         pass
 
-    for copy in log_sends:
-        copy.wait_recv()
+    sent_logs = [logs.at[pl.ds(0, 2 * CHIPS - 1)] for logs in (image_logs, text_logs)]
+    for kind in range(2):
+        all_of(sent_logs[kind], log_recv.at[kind]).wait_recv()
 
     def whole_log(terms):
         top = terms[0]
@@ -416,14 +425,14 @@
         total = sum(jnp.exp2(term - top) for term in terms)
         return top + jnp.log(total) * LOG2_E
 
-    terms = [image_logs[0, offset] for offset in range(CHIPS)]
+    terms = [image_logs[offset] for offset in range(CHIPS)]
     for offset in range(CHIPS):
-        term = image_logs[1, offset]
+        term = image_logs[CHIPS + offset]
         terms.append(jnp.concatenate([term[half_pieces:], term[:half_pieces]], axis=0))
     image_log = whole_log(terms)
     image_log = jnp.concatenate([image_log[piece] for piece in range(PIECES)], axis=1)
     for half in range(2):
-        text_log = whole_log([text_logs[half, offset] for offset in range(CHIPS)])
+        text_log = whole_log([text_logs[half * CHIPS + offset] for offset in range(CHIPS)])
         col_scale = jnp.exp2(col_peak[half] - image_log)
         for piece in range(half_pieces):
             rows = slice(piece * PIECE, (piece + 1) * PIECE)
@@ -434,7 +443,6 @@
             weight[first : first + PIECE, :] = both.astype(BF16)
 
     duty = 1 - core
-    part_sends = []
     for far in (1, 0):
         first = place.slot(duty, 4 * far) // 4 * 4
         spans = [
@@ -458,50 +466,38 @@
             slot = place.slot(duty, offset)
             for side in range(2):
                 if offset == 0 and side == 0:
-                    parts[duty, 0] = blocks[0, slot]
+                    parts[duty * CHIPS] = blocks[0, slot]
                     continue
                 copy = pltpu.make_async_remote_copy(
                     src_ref=blocks.at[side, slot],
-                    dst_ref=parts.at[duty, offset],
-                    send_sem=part_send.at[offset, side],
-                    recv_sem=part_recv.at[duty, offset],
+                    dst_ref=parts.at[duty * CHIPS + offset],
+                    send_sem=part_sem.at[0],
+                    recv_sem=part_sem.at[1],
                     device_id=(place.peer(duty, offset, core + side - 2 * side * core),),
                     device_id_type=MESH,
                 )
                 copy.start()
-                part_sends.append(copy)
-
-    def arrived(kind, offset):
-        pltpu.make_async_remote_copy(
-            src_ref=parts.at[kind, offset],
-            dst_ref=parts.at[kind, offset],
-            send_sem=part_send.at[0, 0],
-            recv_sem=part_recv.at[kind, offset],
-            device_id=(partner,),
-            device_id_type=MESH,
-        ).wait_recv()
-
-    arrived(core, 0)
-    for offset in range(1, CHIPS):
-        for kind in range(2):
-            arrived(kind, offset)
+
+    sent_parts = parts.at[pl.ds(0, 2 * CHIPS - 1)]
+    all_of(sent_parts, part_sem.at[1]).wait_recv()
 
     half = 0.5 * LOGIT_SCALE
     sums = []
     for kind in range(2):
-        total = parts[kind, 0].astype(F32)
+        total = parts[kind * CHIPS].astype(F32)
         for offset in range(1, CHIPS):
-            total = total + parts[kind, offset].astype(F32)
+            total = total + parts[kind * CHIPS + offset].astype(F32)
         sums.append(total)
     image_unit_grad = half * sums[0] - LOGIT_SCALE * text_unit.astype(F32)
     text_unit_grad = half * sums[1] - LOGIT_SCALE * image_unit.astype(F32)
     image_grad[...] = unit_back(image_values, image_unit_grad)
     text_grad[...] = unit_back(text_values, text_unit_grad)
 
-    for copy in [*image_sends.values(), *text_sends.values(), *passed.values()]:
-        copy.wait_send()
-    for copy in log_sends + part_sends:
-        copy.wait_send()
+    for kind in range(2):
+        all_of(units.at[kind, 0, pl.ds(0, CHIPS - 1)], gather_send.at[kind]).wait_send()
+        all_of(units.at[kind, 0], pass_send.at[kind]).wait_send()
+        all_of(sent_logs[kind], log_send.at[kind]).wait_send()
+    all_of(sent_parts, part_sem.at[0]).wait_send()
 
 
 def hand_out(image_from, text_from, image_to, text_to):
@@ -540,22 +536,21 @@
             pltpu.VMEM((2, HALF, ROWS), F32),
             pltpu.VMEM((2, HALF, 1), F32),
             pltpu.VMEM((2, 1, ROWS), F32),
-            pltpu.VMEM((2, CHIPS, PIECES, 1, PIECE), F32),
-            pltpu.VMEM((2, CHIPS, HALF // PIECE, 1, PIECE), F32),
+            pltpu.VMEM((2 * CHIPS, PIECES, 1, PIECE), F32),
+            pltpu.VMEM((2 * CHIPS, HALF // PIECE, 1, PIECE), F32),
             pltpu.VMEM((ROWS, ROWS), BF16),
             pltpu.VMEM((2, CHIPS, CAPS, WIDTH), BF16),
-            pltpu.VMEM((2, CHIPS, CAPS, WIDTH), BF16),
+            pltpu.VMEM((2 * CHIPS, CAPS, WIDTH), BF16),
             dma((3,)),
             dma((LOAD_STEPS + 1,)),
             dma((7,)),
-            dma((2, CHIPS)),
-            dma((2, CHIPS)),
-            dma((2, CHIPS)),
-            dma((2, CHIPS)),
-            dma((2, 2, CHIPS)),
-            dma((2, 2, CHIPS)),
-            dma((CHIPS, 2)),
-            dma((2, CHIPS)),
+            dma((2,)),
+            dma((CHIPS,)),
+            dma((2,)),
+            dma((2,)),
+            dma((2,)),
+            dma((2,)),
+            dma((2,)),
         ],
         compiler_params=pltpu.CompilerParams(
             collective_id=0, has_side_effects=True, vmem_limit_bytes=VMEM_LIMIT

time: 38.1 us -> 36.6 us (0.961)
  Pallas kernels: 37.4 us -> 35.8 us
    pallas_call x1, Pallas kernels: 36.7 us -> 35.2 us  [body(): pl.pallas_call(kernel, out_shape=(pltpu.VMEM((CAPS, WIDTH), F32),) * 2, i...]
where the time goes in v8:
time: 36.6 us; the launch traced here: 36.5 us
  Pallas kernels  35.8 us (98%)
  between operations  0.64 us (2%)
    pallas_call x1, Pallas kernels, body(): pl.pallas_call(kernel, out_shape=(pltpu.VMEM((CAPS, WIDTH), F32),) * 2, i...  35.2 us

profile of v8, /device:TPU:1, one launch (start us, length us, event | category | flops | bytes accessed | tf_op | source)
XLA Modules:
  0.0 36.5 jit_solution(16312253005562364822)
XLA Ops:
  0.6 35.2 %shard_map.104 = (f32[32,768]{1,0:T(8,128)S(1)}, f32[32,768]{1,0:T(8,128)S(1)}) custom-call(bf16[77,32,768]{2,1,0:T(8,128)(2,1)} %bitcast.1, s32[2,4096]{1,0:T(2,128)} %layout.1, bf16[32,768]{1,0:T(8,128)(2,1)} %images.1, bf16[768,768]{1,0:T(8,128)(2,1)} %w_query.1, bf16[768,1536]{1,0:T(8,128)(2,1)} %w_keyval.1, bf16[768,768]{1,0:T(8,128)(2,1)} %w_out.1, ...), custom_call_target="tpu_custom_call" | custom-call | tf_op jit(solution)/shard_map/pallas_call | solution.py:513
  35.8 0.7 %shard_map.105 = (f32[32,768]{1,0:T(8,128)}, f32[32,768]{1,0:T(8,128)}) custom-call(f32[32,768]{1,0:T(8,128)S(1)} %get-tuple-element.4.image_from, f32[32,768]{1,0:T(8,128)S(1)} %get-tuple-element.5.text_from), custom_call_target="tpu_custom_call" | custom-call | tf_op jit(solution)/shard_map/pallas_call | solution.py:569

commit v9 on v8

--- a/solution.py
+++ b/solution.py
@@ -27,7 +27,6 @@
 STEP_T = 12
 TAIL = CTX - LOAD_STEPS * STEP_T
 CHIPS = 8
-ARRIVAL = (7, 1, 6, 3, 2, 5, 4)
 ROWS = CHIPS * 2 * CAPS
 HALF = ROWS // 2
 PIECE = 128
@@ -302,18 +301,16 @@
     pl.semaphore_wait(barrier, len(friends))
 
     def send_units(kind):
-        copies = {}
         for offset in range(CHIPS - 1, 0, -1):
-            copies[offset] = pltpu.make_async_remote_copy(
+            copy = pltpu.make_async_remote_copy(
                 src_ref=units.at[kind, 0, slots[kind]],
                 dst_ref=units.at[kind, 0, slots[kind]],
                 send_sem=gather_send.at[kind],
-                recv_sem=gather_recv.at[offset] if kind else gather_recv.at[0],
+                recv_sem=gather_recv.at[kind],
                 device_id=(place.peer(kind, offset, core),),
                 device_id_type=MESH,
             )
-            copies[offset].start()
-        return copies
+            copy.start()
 
     def hand_on(kind, offset):
         slot = place.slot(kind, offset)
@@ -361,15 +358,15 @@
     text_unit = (text_values * unit_scale(text_values)).astype(BF16)
     units[1, 0, slots[1]] = text_unit
 
-    text_sends = send_units(1)
+    send_units(1)
     hand_on(1, 0)
 
     all_of(units.at[0, 0, pl.ds(0, CHIPS - 1)], gather_recv.at[0]).wait_recv()
     for offset in range(1, CHIPS):
         hand_on(0, offset)
 
-    for offset in ARRIVAL:
-        text_sends[offset].wait_recv()
+    all_of(units.at[1, 0, pl.ds(0, CHIPS - 1)], gather_recv.at[1]).wait_recv()
+    for offset in range(1, CHIPS):
         hand_on(1, offset)
     all_of(units.at[0, 1], pass_recv.at[0]).wait_recv()
 
@@ -545,7 +542,7 @@
             dma((LOAD_STEPS + 1,)),
             dma((7,)),
             dma((2,)),
-            dma((CHIPS,)),
+            dma((2,)),
             dma((2,)),
             dma((2,)),
             dma((2,)),

time: 36.6 us -> 36.5 us (level)
  no operation moved by 1% of the time
where the time goes in v9:
time: 36.5 us; the launch traced here: 36.4 us
  Pallas kernels  35.8 us (98%)
  between operations  0.64 us (2%)
    pallas_call x1, Pallas kernels, body(): pl.pallas_call(kernel, out_shape=(pltpu.VMEM((CAPS, WIDTH), F32),) * 2, i...  35.1 us

profile of v9, /device:TPU:1, one launch (start us, length us, event | category | flops | bytes accessed | tf_op | source)
XLA Modules:
  0.0 36.4 jit_solution(5414451864837273009)
XLA Ops:
  0.6 35.1 %shard_map.104 = (f32[32,768]{1,0:T(8,128)S(1)}, f32[32,768]{1,0:T(8,128)S(1)}) custom-call(bf16[77,32,768]{2,1,0:T(8,128)(2,1)} %bitcast.1, s32[2,4096]{1,0:T(2,128)} %layout.1, bf16[32,768]{1,0:T(8,128)(2,1)} %images.1, bf16[768,768]{1,0:T(8,128)(2,1)} %w_query.1, bf16[768,1536]{1,0:T(8,128)(2,1)} %w_keyval.1, bf16[768,768]{1,0:T(8,128)(2,1)} %w_out.1, ...), custom_call_target="tpu_custom_call" | custom-call | tf_op jit(solution)/shard_map/pallas_call | solution.py:510
  35.8 0.7 %shard_map.105 = (f32[32,768]{1,0:T(8,128)}, f32[32,768]{1,0:T(8,128)}) custom-call(f32[32,768]{1,0:T(8,128)S(1)} %get-tuple-element.4.image_from, f32[32,768]{1,0:T(8,128)S(1)} %get-tuple-element.5.text_from), custom_call_target="tpu_custom_call" | custom-call | tf_op jit(solution)/shard_map/pallas_call | solution.py:566

commit v10 on v9

--- a/solution.py
+++ b/solution.py
@@ -279,7 +279,7 @@
             value = jnp.exp2(value - jnp.max(value, axis=1, keepdims=True))
             attn[group, rows, :] = value.astype(BF16)
             totals.append(jnp.sum(value, axis=1, keepdims=True))
-        context = dot(attn[group], normed[group]) / jnp.concatenate(totals, axis=0)
+        context = dot(attn[group], normed[group]) * (1.0 / jnp.concatenate(totals, axis=0))
         contexts.append(context.astype(BF16))
 
     load_images.wait()

time: 36.5 us -> 36.5 us (level)
  no operation moved by 1% of the time
where the time goes in v10:
time: 36.5 us; the launch traced here: 36.4 us
  Pallas kernels  35.8 us (98%)
  between operations  0.64 us (2%)
    pallas_call x1, Pallas kernels, body(): pl.pallas_call(kernel, out_shape=(pltpu.VMEM((CAPS, WIDTH), F32),) * 2, i...  35.1 us

profile of v10, /device:TPU:1, one launch (start us, length us, event | category | flops | bytes accessed | tf_op | source)
XLA Modules:
  0.0 36.4 jit_solution(10635555750416145465)
XLA Ops:
  0.6 35.1 %shard_map.104 = (f32[32,768]{1,0:T(8,128)S(1)}, f32[32,768]{1,0:T(8,128)S(1)}) custom-call(bf16[77,32,768]{2,1,0:T(8,128)(2,1)} %bitcast.1, s32[2,4096]{1,0:T(2,128)} %layout.1, bf16[32,768]{1,0:T(8,128)(2,1)} %images.1, bf16[768,768]{1,0:T(8,128)(2,1)} %w_query.1, bf16[768,1536]{1,0:T(8,128)(2,1)} %w_keyval.1, bf16[768,768]{1,0:T(8,128)(2,1)} %w_out.1, ...), custom_call_target="tpu_custom_call" | custom-call | tf_op jit(solution)/shard_map/pallas_call | solution.py:510
  35.8 0.7 %shard_map.105 = (f32[32,768]{1,0:T(8,128)}, f32[32,768]{1,0:T(8,128)}) custom-call(f32[32,768]{1,0:T(8,128)S(1)} %get-tuple-element.4.image_from, f32[32,768]{1,0:T(8,128)S(1)} %get-tuple-element.5.text_from), custom_call_target="tpu_custom_call" | custom-call | tf_op jit(solution)/shard_map/pallas_call | solution.py:566
